TPU v7x, 256 devices: a whole 4x4x8 slice. The times are simulated.
256 devices in a mesh: tm: 128 (over z, y, x_lo, core), gen: 2 (over x_hi).
Axes of the slice: x: 4 (x_hi: 2, x_lo: 2; x = x_hi * 2 + x_lo), y: 4, z: 8, core: 2. Of those that a mesh axis runs over, the one named last changes fastest.
Arguments:
- dispatch: float32 [12288, 8192], P('tm', 'gen'), may hold values from 0 to 2
- cost: float32 [8192], P('gen'), may hold values from -4 to 4
- p_low: float32 [8192], P('gen'), may hold values from 0 to 0.4
- p_high: float32 [8192], P('gen'), may hold values from 1.2 to 2.5
- ramp_limit: float32 [8192], P('gen'), may hold values from 0.05 to 1
- p_init: float32 [8192], P('gen'), may hold values from 0 to 2
- demand: float32 [12288], P('tm'), may hold values from 70 to 110
- bus_of: int32 [8192], P('gen'), may hold values from 0 to 2047
- ptdf: bfloat16 [1024, 2048], replicated, may hold values from -0.0625 to 0.0625
- line_base: float32 [12288, 1024], P('tm', 'gen'), may hold values from -6 to 6
- line_limit: float32 [1024], P('gen'), may hold values from 0.2 to 2
- line_dual: float32 [12288, 1024], P('tm', 'gen'), may hold values from -3 to 3
- ramp_dual: float32 [12288, 8192], P('tm', 'gen'), may hold values from -3 to 3
- balance_dual: float32 [12288], P('tm'), may hold values from -5 to 5
Outputs:
- dispatch_out: float32 [12288, 8192], P('tm', 'gen')
- line_dual_out: float32 [12288, 1024], P('tm', 'gen')
- ramp_dual_out: float32 [12288, 8192], P('tm', 'gen')
- balance_dual_out: float32 [12288], P('tm')
- movement: float32 [2, 2], replicated
Inputs may be any that keep to these rules, and one draw needn't show every extreme that they name: `bus_of`: each generator's bus.
All inputs are finite; a program needn't handle non-finite values.
Results may differ from a plain program's by a relative error of at most 0.0011.
Values may be sent and summed in bfloat16 or wider, within the bound.
A program may use at most 64 MiB of HBM per device.

v0:
```python
import functools
import math

import jax
import jax.numpy as jnp
from jax import lax
from jax.sharding import Mesh
from jax.sharding import PartitionSpec as P

G = 8192
ITERS = 2
TM = ("tm_0", "tm_1", "tm_2", "tm_3")
TM_GEN = ("tm_0", "tm_1", "tm_2", "tm_3", "gen")


TAU = 0.35
SIGMA = 0.35


def laid_out(parts, dim):
    parts = jnp.moveaxis(parts, 0, dim)
    dims = parts.shape
    return parts.reshape(*dims[:dim], dims[dim] * dims[dim + 1], *dims[dim + 2 :])


def sent_to_all(array, axis):
    peers = lax.axis_size(axis)
    return lax.all_to_all(
        jnp.broadcast_to(array[None], (peers, *array.shape)), axis, 0, 0, tiled=True
    )


def gather_directly(array, axis, dim):
    return laid_out(sent_to_all(array, axis), dim)


def in_one_piece(arrays, axis, dim, along):
    ends, at = ([], 0)
    for a in arrays[:-1]:
        at += a.shape[along]
        ends.append(at)
    both = jnp.concatenate(arrays, axis=along)
    return tuple(jnp.split(gather_directly(both, axis, dim), ends, axis=along))


def passed_along(block, axis, distance):
    devices = range(lax.axis_size(axis))
    route = [(i - distance, i) for i in devices if i - distance in devices]
    return lax.ppermute(block, axis, route)


def over_copies(array, axis):
    everything = sent_to_all(array, axis)
    return jnp.sum(everything, axis=0)


def packed_total(arrays, axis):
    vector, at, finished = (jnp.concatenate([a.reshape(-1) for a in arrays]), 0, [])
    subtotal = over_copies(vector, axis)
    for a in arrays:
        finished.append(subtotal[at : at + a.size].reshape(a.shape))
        at += a.size
    return tuple(finished)


def over_axes(array, axes):
    return functools.reduce(lax.psum, axes, array)


def on_device(
    dispatch,
    cost,
    p_low,
    p_high,
    ramp_limit,
    p_init,
    demand,
    bus_of,
    ptdf,
    line_base,
    line_limit,
    line_dual,
    ramp_dual,
    balance_dual,
):
    rows = dispatch.shape[0]
    half_lines = line_dual.shape[1]
    gen_pos = lax.axis_index("gen")
    first_block = lax.axis_index(TM) == 0
    weight_bal = 1.0 / math.sqrt(G)
    cells = float(rows * lax.axis_size(TM)) * float(G)
    columns = jnp.take(ptdf, bus_of, axis=1)
    duals, base_rows, limit_rows = (
        *in_one_piece((line_dual, line_base), "gen", 1, 0),
        gather_directly(line_limit, "gen", 0),
    )
    low_side = base_rows - limit_rows[None, :]
    high_side = base_rows + limit_rows[None, :]
    state_x = dispatch
    ramp_mult = ramp_dual
    balance = balance_dual
    records = []
    for step in range(ITERS):
        rounded = duals.astype(jnp.bfloat16)
        pulled = jnp.dot(rounded, columns, preferred_element_type=jnp.float32)
        next_row = passed_along(ramp_mult[:1], TM, -1)
        after = jnp.concatenate([ramp_mult[1:], next_row], 0)
        grad = cost[None, :] + weight_bal * balance[:, None] + pulled + ramp_mult - after
        x_new = jnp.clip(state_x - TAU * grad, p_low[None, :], p_high[None, :])
        xbar = 2.0 * x_new - state_x
        flow_part = lax.dot_general(
            xbar.astype(jnp.bfloat16),
            columns,
            (((1,), (1,)), ((), ())),
            preferred_element_type=jnp.float32,
        )
        total_part = weight_bal * jnp.sum(xbar, axis=1)
        flows, totals = packed_total((flow_part, total_part), "gen")
        balance_new = balance + SIGMA * (totals - demand)
        moved = duals + SIGMA * flows
        duals_new = moved - SIGMA * jnp.clip(moved / SIGMA, low_side, high_side)
        prev_row = passed_along(xbar[-1:], TM, 1)
        prev_row = jnp.where(first_block, p_init[None, :], prev_row)
        before = jnp.concatenate([prev_row, xbar[:-1]], 0)
        shifted = ramp_mult + SIGMA * (xbar - before)
        ramp_new = shifted - SIGMA * jnp.clip(
            shifted / SIGMA, -ramp_limit[None, :], ramp_limit[None, :]
        )
        primal_step = x_new - state_x
        dual_step = duals_new - duals
        dual_step = lax.dynamic_slice_in_dim(dual_step, gen_pos * half_lines, half_lines, 1)
        ramp_step = ramp_new - ramp_mult
        balance_step = balance_new - balance
        balance_term = jnp.where(gen_pos == 0, jnp.sum(balance_step * balance_step), 0.0)
        primal = jnp.sum(primal_step * primal_step) / (TAU * cells)
        dual = (jnp.sum(dual_step * dual_step) + jnp.sum(ramp_step * ramp_step) + balance_term) / (
            SIGMA * cells
        )
        paired = jnp.stack([primal, dual])
        paired = over_axes(paired, TM_GEN)
        records.append(paired)
        state_x, duals, ramp_mult, balance = (x_new, duals_new, ramp_new, balance_new)
    movement = jnp.stack(records)
    duals = lax.dynamic_slice_in_dim(duals, gen_pos * half_lines, half_lines, 1)
    return (state_x, duals, ramp_mult, balance, movement)


def solution(mesh):
    finer = Mesh(
        mesh.devices.reshape(8, 4, 2, 2, mesh.shape["gen"]), ("tm_0", "tm_1", "tm_2", "tm_3", "gen")
    )
    in_specs = (
        P(TM, "gen"),
        P("gen"),
        P("gen"),
        P("gen"),
        P("gen"),
        P("gen"),
        P(TM),
        P("gen"),
        P(),
        P(TM, "gen"),
        P("gen"),
        P(TM, "gen"),
        P(TM, "gen"),
        P(TM),
    )
    out_specs = (P(TM, "gen"), P(TM, "gen"), P(TM, "gen"), P(TM), P())
    return jax.shard_map(
        on_device, mesh=finer, in_specs=in_specs, out_specs=out_specs, check_vma=False
    )
```

profile of v0, /device:TPU:1, one launch (start us, length us, event | category | flops | bytes accessed | tf_op | source)
XLA Modules:
  0.0 175.1 jit_solution(12164860447620574211)
XLA Ops:
  0.6 1.0 pad_maximum_fusion.2
  1.7 1.0 broadcast_in_dim.22
  2.7 4.8 %all-to-all-start = ((f32[2,192,512]{2,1,0:T(8,128)}), f32[2,192,512]{2,1,0:T(8,128)S(1)}, u32[]{:S(2)}, u32[]{:S(2)}) async-start(f32[2,192,512]{2,1,0:T(8,128)} %broadcast_in_dim.22), calls=%async_computation | async-start | bytes 1572864 | tf_op jit(solution)/shard_map/all_to_all | solution.py:28
  7.5 3.8 %collective-permute-start = (f32[1,4096]{1,0:T(1,128)S(1)}, f32[1,4096]{1,0:T(1,128)S(1)}, u32[]{:S(2)}, u32[]{:S(2)}) collective-permute-start(f32[1,4096]{1,0:T(1,128)S(1)} %slice.39), channel_id=1, source_target_pairs={{2,0},{4,2},{6,4},{8,6},{10,8},{12,10},{14,12},{16,14},{18,16},{20... | collective-permute-start | bytes 49160 | tf_op jit(solution)/shard_map/ppermute | solution.py:49
  11.4 1.3 slice.38
  12.6 6.4 %copy.28 = bf16[1024,2048]{0,1:T(8,128)(2,1)} copy(bf16[1024,2048]{1,0:T(8,128)(2,1)} %param.22) | data formatting | bytes 8388608 | tf_op args[8]
  19.1 0.6 neg.5
  19.7 23.6 %gather_fusion = bf16[4096,1024]{1,0:T(8,128)(2,1)} fusion(bf16[1024,2048]{0,1:T(8,128)(2,1)} %copy.28, s32[4096]{0:T(1024)S(1)} %fusion.20), kind=kCustom, calls=%fused_computation | custom fusion | bytes 16793600 | tf_op jit(solution)/shard_map/jit(_take)/gather | solution.py:92
  43.4 0.8 slice_bitcast_fusion
  44.3 0.6 copy-done.7
  44.9 7.4 %fusion.28 = (f32[96]{0:T(128)S(1)}, f32[96,4096]{1,0:T(8,128)S(1)}, f32[96,4096]{1,0:T(8,128)}) fusion(f32[96,4096]{1,0:T(8,128)} %param.14, f32[1,4096]{1,0:T(1,128)S(1)} %collective-permute-done, f32[95,4096]{1,0:T(8,128)S(1)} %copy-done.7, f32[96,4096]{1,0:T(8,128)S(1)} %copy-done, bf16[4096,1024]{1,0:T(8,128)(2,1)} %gather_fusion, ...), kind=kOutput, calls=%fused_computation.71 | convolution fusion | flops 814317440 | bytes 16700160 | tf_op jit(solution)/shard_map/dot_general | solution.py:105
  52.4 0.7 slice.54
  53.1 1.7 convolution_bitcast_fusion.1
  54.8 1.9 %collective-permute-start.1 = (f32[1,4096]{1,0:T(1,128)}, f32[1,4096]{1,0:T(1,128)}, u32[]{:S(2)}, u32[]{:S(2)}) collective-permute-start(f32[1,4096]{1,0:T(1,128)} %slice.54), channel_id=1, source_target_pairs={{0,2},{2,4},{4,6},{6,8},{8,10},{10,12},{12,14},{14,16},{16,18},{18... | collective-permute-start | bytes 49160 | tf_op jit(solution)/shard_map/ppermute | solution.py:49
  56.8 1.3 broadcast_in_dim.26
  58.1 4.5 %all-to-all-start.1 = ((f32[2,1,98400]{2,1,0:T(1,128)}), f32[2,1,98400]{2,1,0:T(1,128)}, u32[]{:S(2)}, u32[]{:S(2)}) async-start(f32[2,1,98400]{2,1,0:T(1,128)} %broadcast_in_dim.26), calls=%async_computation.1 | async-start | bytes 1574912 | tf_op jit(solution)/shard_map/all_to_all | solution.py:28
  62.7 0.7 broadcast_select_fusion.2
  63.4 2.4 %multiply_subtract_fusion.2 = f32[96,4096]{1,0:T(8,128)S(1)} fusion(f32[96,4096]{1,0:T(8,128)S(1)} %copy-done, f32[96,4096]{1,0:T(8,128)} %copy-done.2, f32[95,4096]{1,0:T(8,128)} %bitcast.28, f32[1,4096]{1,0:T(1,128)S(1)} %broadcast_select_fusion.2, f32[4096]{0:T(1024)} %neg.5, f32[4096]{0:T(1024)S(1)} %copy-done.10), kind=kLoop, calls=%fused_computation.28 | loop fusion | flops 3538944 | bytes 6324224 | tf_op jit(solution)/shard_map/sub | solution.py:126
  65.8 1.3 slice.56
  67.1 0.6 slice.57
  67.7 2.5 %collective-permute-start.2 = (f32[1,4096]{1,0:T(1,128)}, f32[1,4096]{1,0:T(1,128)}, u32[]{:S(2)}, u32[]{:S(2)}) collective-permute-start(f32[1,4096]{1,0:T(1,128)} %slice.57), channel_id=1, source_target_pairs={{2,0},{4,2},{6,4},{8,6},{10,8},{12,10},{14,12},{16,14},{18,16},{20... | collective-permute-start | bytes 49160 | tf_op jit(solution)/shard_map/ppermute | solution.py:49
  70.3 3.7 %all-to-all-done.1 = f32[2,1,98400]{2,1,0:T(1,128)} async-done(((f32[2,1,98400]{2,1,0:T(1,128)}), f32[2,1,98400]{2,1,0:T(1,128)}, u32[]{:S(2)}, u32[]{:S(2)}) %all-to-all-start.1) | async-done | bytes 787232 | tf_op jit(solution)/shard_map/all_to_all | solution.py:28
  74.0 1.3 broadcast_in_dim.27
  75.3 3.8 %all-to-all-start.2 = ((f32[2,1,512]{2,1,0:T(1,128)}), f32[2,1,512]{2,1,0:T(1,128)}, u32[]{:S(2)}, u32[]{:S(2)}) async-start(f32[2,1,512]{2,1,0:T(1,128)} %broadcast_in_dim.27), calls=%async_computation.2 | async-start | bytes 8192 | tf_op jit(solution)/shard_map/all_to_all | solution.py:28
  79.1 3.1 %reduce_sum.109 = f32[98400]{0:T(1024)} reduce(f32[2,1,98400]{2,1,0:T(1,128)} %all-to-all-done.1, f32[]{:T(128)} %constant.55.clone.1), dimensions={0,1}, to_apply=%region_1.2 | reduce | flops 98400 | bytes 1180804 | tf_op jit(solution)/shard_map/reduce_sum | solution.py:54
  82.1 1.8 %slice_multiply_fusion.1 = f32[98304]{0:T(1024)} fusion(f32[98400]{0:T(1024)} %reduce_sum.109), kind=kLoop, calls=%fused_computation.38 | loop fusion | flops 98304 | bytes 786432 | tf_op jit(solution)/shard_map/mul | solution.py:120
  84.0 1.8 %mul.107 = f32[96,1024]{1,0:T(8,128)} reshape(f32[98304]{0:T(1024)} %slice_multiply_fusion.1) | data formatting | bytes 786432 | tf_op jit(solution)/shard_map/mul | solution.py:120
  85.8 1.4 multiply_subtract_fusion.5
  87.2 1.9 %broadcast_multiply_fusion.1 = (f32[96]{0:T(128)S(1)}, f32[96]{0:T(128)}) fusion(f32[96]{0:T(128)S(1)} %copy-done.16, f32[96]{0:T(128)S(1)} %copy-done.18, f32[98400]{0:T(1024)} %reduce_sum.109), kind=kLoop, calls=%fused_computation.67 | loop fusion | flops 384 | bytes 1920 | tf_op jit(solution)/shard_map/mul | solution.py:108
  89.1 7.6 %multiply_reduce_fusion.3 = (f32[]{:T(128)}, f32[]{:T(128)}, f32[96]{0:T(128)S(1)}, f32[96,4096]{1,0:T(8,128)S(1)}, f32[96,4096]{1,0:T(8,128)}) fusion(f32[96,4096]{1,0:T(8,128)} %get-tuple-element.36, f32[96,4096]{1,0:T(8,128)} %param.14, f32[1,4096]{1,0:T(1,128)} %collective-permute-done.2, f32[95,4096]{1,0:T(8,128)S(1)} %copy-done.8, ...), kind=kOutput, calls=%fused_computation.25 | convolution fusion | flops 816676736 | bytes 18273032 | tf_op jit(solution)/shard_map/dot_general | solution.py:105
  96.7 0.7 slice.59
  97.4 1.6 convolution_bitcast_fusion
  99.0 3.9 %collective-permute-start.3 = (f32[1,4096]{1,0:T(1,128)}, f32[1,4096]{1,0:T(1,128)}, u32[]{:S(2)}, u32[]{:S(2)}) collective-permute-start(f32[1,4096]{1,0:T(1,128)} %slice.59), channel_id=1, source_target_pairs={{0,2},{2,4},{4,6},{6,8},{8,10},{10,12},{12,14},{14,16},{16,18},{18... | collective-permute-start | bytes 49160 | tf_op jit(solution)/shard_map/ppermute | solution.py:49
  103.1 1.3 broadcast_in_dim.29
  104.4 5.1 %all-to-all-start.3 = ((f32[2,1,98400]{2,1,0:T(1,128)}), f32[2,1,98400]{2,1,0:T(1,128)}, u32[]{:S(2)}, u32[]{:S(2)}) async-start(f32[2,1,98400]{2,1,0:T(1,128)} %broadcast_in_dim.29), calls=%async_computation.3 | async-start | bytes 1574912 | tf_op jit(solution)/shard_map/all_to_all | solution.py:28
  110.8 0.8 broadcast_select_fusion.1
  111.5 4.5 %multiply_reduce_fusion.2 = (f32[]{:T(128)}, f32[]{:T(128)}, f32[96,4096]{1,0:T(8,128)}) fusion(f32[96,4096]{1,0:T(8,128)S(1)} %multiply_subtract_fusion.2, f32[96,4096]{1,0:T(8,128)S(1)} %copy-done, f32[4096]{0:T(1024)} %neg.5, f32[4096]{0:T(1024)S(1)} %copy-done.10, f32[96,4096]{1,0:T(8,128)} %copy-done.1, f32[95,4096]{1,0:T(8,128)} %bitcast.27, ...), kind=kLoop, calls=%fused_computation.24 | loop fusion | flops 5898238 | bytes 7897096 | tf_op jit(solution)/shard_map/reduce_sum | solution.py:136
  116.0 6.5 %all-to-all-done.3 = f32[2,1,98400]{2,1,0:T(1,128)} async-done(((f32[2,1,98400]{2,1,0:T(1,128)}), f32[2,1,98400]{2,1,0:T(1,128)}, u32[]{:S(2)}, u32[]{:S(2)}) %all-to-all-start.3) | async-done | bytes 787232 | tf_op jit(solution)/shard_map/all_to_all | solution.py:28
  122.5 2.3 %reduce_sum.111 = f32[98400]{0:T(1024)S(1)} reduce(f32[2,1,98400]{2,1,0:T(1,128)} %all-to-all-done.3, f32[]{:T(128)} %constant.55.clone.1), dimensions={0,1}, to_apply=%region_3.4 | reduce | flops 98400 | bytes 1180804 | tf_op jit(solution)/shard_map/reduce_sum | solution.py:54
  125.0 0.8 multiply_subtract_fusion.4
  125.8 1.2 multiply_reduce_fusion.6
  127.0 1.3 fusion.17
  132.1 14.8 %all-reduce = (f32[2]{0:T(128)S(1)}, f32[2]{0:T(128)S(1)}) all-reduce(f32[2]{0:T(128)S(1)} %get-tuple-element.39, f32[2]{0:T(128)S(1)} %get-tuple-element.38), channel_id=1, replica_groups=mesh['tm_0'=8,'tm_1'=4,'tm_2'=2,'tm_3'=2,'gen'=2] {'tm_0'}, use_global_device_ids=true, to_apply=%region_17.18 | all-reduce | flops 4 | bytes 32 | tf_op jit(solution)/shard_map/psum | solution.py:67
  146.9 8.8 %all-reduce.1 = (f32[2]{0:T(128)S(1)}, f32[2]{0:T(128)S(1)}) all-reduce(f32[2]{0:T(128)S(1)} %get-tuple-element.13, f32[2]{0:T(128)S(1)} %get-tuple-element.14), channel_id=1, replica_groups=mesh['tm_0'=8,'tm_1'=4,'tm_2'=2,'tm_3'=2,'gen'=2] {'tm_1'}, use_global_device_ids=true, to_apply=%region_18.19 | all-reduce | flops 4 | bytes 32 | tf_op jit(solution)/shard_map/psum | solution.py:67
  155.7 3.8 %all-reduce.4 = (f32[2]{0:T(128)S(1)}, f32[2]{0:T(128)S(1)}) all-reduce(f32[2]{0:T(128)S(1)} %get-tuple-element.15, f32[2]{0:T(128)S(1)} %get-tuple-element.16), channel_id=1, replica_groups=mesh['tm_0'=8,'tm_1'=4,'tm_2'=2,'tm_3'=2,'gen'=2] {'tm_2'}, use_global_device_ids=true, to_apply=%region_19.20 | all-reduce | flops 4 | bytes 32 | tf_op jit(solution)/shard_map/psum | solution.py:67
  159.4 9.8 %all-reduce.3 = (f32[2]{0:T(128)S(1)}, f32[2]{0:T(128)S(1)}) all-reduce(f32[2]{0:T(128)S(1)} %get-tuple-element.21, f32[2]{0:T(128)S(1)} %get-tuple-element.22), channel_id=1, replica_groups=mesh['tm_0'=8,'tm_1'=4,'tm_2'=2,'tm_3'=2,'gen'=2] {'tm_3'}, use_global_device_ids=true, to_apply=%region_20.21 | all-reduce | flops 4 | bytes 32 | tf_op jit(solution)/shard_map/psum | solution.py:67
  169.3 5.3 %all-reduce.2 = (f32[1,2]{1,0:T(1,128)S(1)}, f32[1,2]{1,0:T(1,128)S(1)}) all-reduce(f32[1,2]{1,0:T(1,128)S(1)} %bitcast.39, f32[1,2]{1,0:T(1,128)S(1)} %bitcast.40), channel_id=1, replica_groups=mesh['tm_0'=8,'tm_1'=4,'tm_2'=2,'tm_3'=2,'gen'=2] {'gen'}, use_global_device_ids=true, to_apply=%region_21.22 | all-reduce | flops 4 | bytes 32 | tf_op jit(solution)/shard_map/psum | solution.py:67
  174.5 0.6 pad_maximum_fusion.3
  (78 shorter events, 0.6 us)
Async XLA Ops:
  1.7 5.8 %copy-start = (f32[96,4096]{1,0:T(8,128)S(1)}, f32[96,4096]{1,0:T(8,128)}, u32[]{:S(2)}) copy-start(f32[96,4096]{1,0:T(8,128)} %param.26) | copy-start | bytes 4718596
  2.7 40.7 %all-to-all-start = ((f32[2,192,512]{2,1,0:T(8,128)}), f32[2,192,512]{2,1,0:T(8,128)S(1)}, u32[]{:S(2)}, u32[]{:S(2)}) async-start(f32[2,192,512]{2,1,0:T(8,128)} %broadcast_in_dim.22), calls=%async_computation | async-start | bytes 1572864 | tf_op jit(solution)/shard_map/all_to_all | solution.py:28
  7.5 36.8 %collective-permute-start = (f32[1,4096]{1,0:T(1,128)S(1)}, f32[1,4096]{1,0:T(1,128)S(1)}, u32[]{:S(2)}, u32[]{:S(2)}) collective-permute-start(f32[1,4096]{1,0:T(1,128)S(1)} %slice.39), channel_id=1, source_target_pairs={{2,0},{4,2},{6,4},{8,6},{10,8},{12,10},{14,12},{16,14},{18,16},{20... | collective-permute-start | bytes 49160 | tf_op jit(solution)/shard_map/ppermute | solution.py:49
  12.6 6.4 %copy-start.12 = (s32[4096]{0:T(1024)S(1)}, s32[4096]{0:T(1024)}, u32[]{:S(2)}) copy-start(s32[4096]{0:T(1024)} %param.21) | copy-start | bytes 49156
  12.6 6.4 %copy-start.10 = (f32[4096]{0:T(1024)S(1)}, f32[4096]{0:T(1024)}, u32[]{:S(2)}) copy-start(f32[4096]{0:T(1024)} %param.18) | copy-start | bytes 49156
  19.7 23.6 %copy-start.15 = (f32[96]{0:T(128)S(1)}, f32[96]{0:T(128)}, u32[]{:S(2)}) copy-start(f32[96]{0:T(128)} %param.27) | copy-start | bytes 1156
  43.3 1.0 copy-start.21
  43.3 1.0 copy-start.22
  43.3 1.0 copy-start.23
  43.4 9.7 %copy-start.13 = (pred[4096]{0:T(1024)(128)(4,1)}, pred[4096]{0:T(1024)(128)(4,1)S(1)}, u32[]{:S(2)}) copy-start(pred[4096]{0:T(1024)(128)(4,1)S(1)} %compare_and_fusion) | copy-start | bytes 12292
  43.4 1.6 copy-start.7
  44.2 8.8 %slice-start = ((s8[8388608]{0:T(1024)(128)(4,1)}), s8[4194304]{0:T(1024)(128)(4,1)S(1)}, s32[]{:S(2)}) async-start(s8[8388608]{0:T(1024)(128)(4,1)} %bitcast.23), calls=%async_computation.4 | async-start | bytes 8388608
  44.3 8.1 %copy-start.3 = (f32[2,12,8,512]{3,2,0,1:T(8,128)}, f32[2,12,8,512]{3,2,0,1:T(8,128)S(1)}, u32[]{:S(2)}) copy-start(f32[2,12,8,512]{3,2,0,1:T(8,128)S(1)} %copy.38) | copy-start | bytes 1179652
  44.9 8.1 %slice-start.1 = ((s8[8388608]{0:T(1024)(128)(4,1)}), s8[4194304]{0:T(1024)(128)(4,1)S(1)}, s32[]{:S(2)}) async-start(s8[8388608]{0:T(1024)(128)(4,1)} %bitcast.23), calls=%async_computation.5 | async-start | bytes 8388608
  52.4 2.4 %copy-start.2 = (f32[96,4096]{1,0:T(8,128)}, f32[96,4096]{1,0:T(8,128)S(1)}, u32[]{:S(2)}) copy-start(f32[96,4096]{1,0:T(8,128)S(1)} %get-tuple-element.31) | copy-start | bytes 4718596
  54.8 7.9 %collective-permute-start.1 = (f32[1,4096]{1,0:T(1,128)}, f32[1,4096]{1,0:T(1,128)}, u32[]{:S(2)}, u32[]{:S(2)}) collective-permute-start(f32[1,4096]{1,0:T(1,128)} %slice.54), channel_id=1, source_target_pairs={{0,2},{2,4},{4,6},{6,8},{8,10},{10,12},{12,14},{14,16},{16,18},{18... | collective-permute-start | bytes 49160 | tf_op jit(solution)/shard_map/ppermute | solution.py:49
  56.8 5.8 %copy-start.9 = (f32[2,12,8,512]{3,2,1,0:T(8,128)S(1)}, f32[2,12,8,512]{3,2,1,0:T(8,128)}, u32[]{:S(2)}) copy-start(f32[2,12,8,512]{3,2,1,0:T(8,128)} %get-tuple-element.34) | copy-start | bytes 1179652
  56.8 5.8 %copy-start.11 = (f32[4096]{0:T(1024)S(1)}, f32[4096]{0:T(1024)}, u32[]{:S(2)}) copy-start(f32[4096]{0:T(1024)} %param.19) | copy-start | bytes 49156
  58.1 15.9 %all-to-all-start.1 = ((f32[2,1,98400]{2,1,0:T(1,128)}), f32[2,1,98400]{2,1,0:T(1,128)}, u32[]{:S(2)}, u32[]{:S(2)}) async-start(f32[2,1,98400]{2,1,0:T(1,128)} %broadcast_in_dim.26), calls=%async_computation.1 | async-start | bytes 1574912 | tf_op jit(solution)/shard_map/all_to_all | solution.py:28
  67.7 21.4 %collective-permute-start.2 = (f32[1,4096]{1,0:T(1,128)}, f32[1,4096]{1,0:T(1,128)}, u32[]{:S(2)}, u32[]{:S(2)}) collective-permute-start(f32[1,4096]{1,0:T(1,128)} %slice.57), channel_id=1, source_target_pairs={{2,0},{4,2},{6,4},{8,6},{10,8},{12,10},{14,12},{16,14},{18,16},{20... | collective-permute-start | bytes 49160 | tf_op jit(solution)/shard_map/ppermute | solution.py:49
  75.3 10.5 %all-to-all-start.2 = ((f32[2,1,512]{2,1,0:T(1,128)}), f32[2,1,512]{2,1,0:T(1,128)}, u32[]{:S(2)}, u32[]{:S(2)}) async-start(f32[2,1,512]{2,1,0:T(1,128)} %broadcast_in_dim.27), calls=%async_computation.2 | async-start | bytes 8192 | tf_op jit(solution)/shard_map/all_to_all | solution.py:28
  85.8 1.4 copy-start.16
  85.8 1.4 copy-start.18
  85.8 3.3 %copy-start.8 = (f32[95,4096]{1,0:T(8,128)S(1)}, f32[95,4096]{1,0:T(8,128)}, u32[]{:S(2)}) copy-start(f32[95,4096]{1,0:T(8,128)} %slice.56) | copy-start | bytes 4669444
  85.8 3.3 %copy-start.14 = (pred[4096]{0:T(1024)(128)(4,1)S(1)}, pred[4096]{0:T(1024)(128)(4,1)}, u32[]{:S(2)}) copy-start(pred[4096]{0:T(1024)(128)(4,1)} %copy-done.13) | copy-start | bytes 12292
  85.8 11.6 %slice-start.2 = ((s8[8388608]{0:T(1024)(128)(4,1)}), s8[4194304]{0:T(1024)(128)(4,1)S(1)}, s32[]{:S(2)}) async-start(s8[8388608]{0:T(1024)(128)(4,1)} %bitcast.25), calls=%async_computation.6 | async-start | bytes 8388608
  87.2 9.5 %copy-start.5 = (f32[96,1024]{1,0:T(8,128)}, f32[96,1024]{1,0:T(8,128)S(1)}, u32[]{:S(2)}) copy-start(f32[96,1024]{1,0:T(8,128)S(1)} %multiply_subtract_fusion.5) | copy-start | bytes 1179652
  89.1 8.3 %slice-start.3 = ((s8[8388608]{0:T(1024)(128)(4,1)}), s8[4194304]{0:T(1024)(128)(4,1)S(1)}, s32[]{:S(2)}) async-start(s8[8388608]{0:T(1024)(128)(4,1)} %bitcast.25), calls=%async_computation.7 | async-start | bytes 8388608
  96.7 2.3 %copy-start.1 = (f32[96,4096]{1,0:T(8,128)}, f32[96,4096]{1,0:T(8,128)S(1)}, u32[]{:S(2)}) copy-start(f32[96,4096]{1,0:T(8,128)S(1)} %get-tuple-element.33) | copy-start | bytes 4718596
  99.0 11.8 %collective-permute-start.3 = (f32[1,4096]{1,0:T(1,128)}, f32[1,4096]{1,0:T(1,128)}, u32[]{:S(2)}, u32[]{:S(2)}) collective-permute-start(f32[1,4096]{1,0:T(1,128)} %slice.59), channel_id=1, source_target_pairs={{0,2},{2,4},{4,6},{6,8},{8,10},{10,12},{12,14},{14,16},{16,18},{18... | collective-permute-start | bytes 49160 | tf_op jit(solution)/shard_map/ppermute | solution.py:49
  104.4 18.1 %all-to-all-start.3 = ((f32[2,1,98400]{2,1,0:T(1,128)}), f32[2,1,98400]{2,1,0:T(1,128)}, u32[]{:S(2)}, u32[]{:S(2)}) async-start(f32[2,1,98400]{2,1,0:T(1,128)} %broadcast_in_dim.29), calls=%async_computation.3 | async-start | bytes 1574912 | tf_op jit(solution)/shard_map/all_to_all | solution.py:28
  116.0 9.0 %copy-start.6 = (f32[96,1024]{1,0:T(8,128)S(1)}, f32[96,1024]{1,0:T(8,128)}, u32[]{:S(2)}) copy-start(f32[96,1024]{1,0:T(8,128)} %copy-done.5) | copy-start | bytes 1179652
  124.8 1.0 copy-start.17
  124.8 1.0 copy-start.19
  124.8 1.0 copy-start.20
  124.9 2.2 %copy-start.4 = (f32[2,12,8,512]{3,2,0,1:T(8,128)S(1)}, f32[2,12,8,512]{3,2,0,1:T(8,128)}, u32[]{:S(2)}) copy-start(f32[2,12,8,512]{3,2,0,1:T(8,128)} %copy-done.3) | copy-start | bytes 1179652
where the time goes:
time: 176 us; the launch traced here: 175 us
  local copies, waits for them, and re-layouts  43.1 us (24%)
  blocking collectives  42.4 us (24%)
  starting transfers between devices  30.4 us (17%)
  other arithmetic  24.5 us (14%)
  matrix products  18.3 us (10%)
  waiting for transfers between devices  10.2 us (6%)
  between operations  6.06 us (3%)
    psum x5, blocking collectives, over_axes(): return functools.reduce(lax.psum, axes, array)  42.4 us
    gather x1, local copies, waits for them, and re-layouts, on_device(): columns = jnp.take(ptdf, bus_of, axis=1)  23.6 us
    all_to_all x4, starting transfers between devices, sent_to_all(): lax.all_to_all(jnp.broadcast_to(array[None], (peers, *array.shape)), axis...  18.2 us
    dot_general x2, matrix products, on_device(): pulled = jnp.dot(rounded, columns, preferred_element_type=jnp.float32)  15 us
    ppermute x4, starting transfers between devices, passed_along(): return lax.ppermute(block, axis, route)  12.2 us
    all_to_all x4, waiting for transfers between devices, sent_to_all(): lax.all_to_all(jnp.broadcast_to(array[None], (peers, *array.shape)), axis...  10.2 us
    unnamed x60, local copies, waits for them, and re-layouts  8.15 us
    reduce_sum x2, other arithmetic, over_copies(): return jnp.sum(everything, axis=0)  5.33 us
  transfers between devices with their start and end apart: 8, of which 2 were waited for; matrix products, arithmetic and copies ran while one was open for 33% of the time, Pallas kernels for 0%

commit v1 on v0

v1 whole, which is shorter than its diff:
```python
import functools
import math

import jax
import jax.numpy as jnp
from jax import lax
from jax.experimental import pallas as pl
from jax.experimental.pallas import tpu as pltpu
from jax.sharding import PartitionSpec as P

TAU = 0.35
SIGMA = 0.35
ITERS = 2
PLANE = 16
MESH = pl.DeviceIdType.MESH
BF16 = jnp.bfloat16
F32 = jnp.float32


def kernel(
    cfg,
    bus, x_h, cost_h, lo_h, hi_h, ramp_h, pinit_h, dem_h, ptdf_h, base_h, lim_h, y_h, mu_h, lam_h,
    xo_h, yo_h, muo_h, lam_o, mov_o,
    ptdf, table, stage, fac, xv, muv, xbv, xbb, yv, basev, flow_own, yb, fsend, frecv,
    cost, lo, hi, ramp, pinit, lim, dem, lam, mu_next, xb_prev, xb_next,
    acc_p, acc_d, acc_t, msg, ar_a, ar_b,
    load_sem, ptdf_sem, out_sem, yb_send, yb_recv, f_send, f_recv, row_send, row_recv, ar_send, ar_recv,
):
    ntm, plane, gl_total, hours = cfg
    rows, gl = x_h.shape
    lines, buses = ptdf_h.shape
    half = lines // 2
    nz = ntm // plane
    w = 1.0 / math.sqrt(gl_total)
    cells = float(hours) * float(gl_total)
    tm = lax.axis_index("tm")
    gen = lax.axis_index("gen")
    other = 1 - gen
    partner = (tm, other)
    nxt = (lax.rem(tm + 1, ntm), gen)
    prv = (lax.rem(tm + ntm - 1, ntm), gen)
    zz = tm // plane
    in_plane = lax.rem(tm, plane)
    n_a = 2 * plane
    mine_a = in_plane * 2 + gen

    def peer_a(d):
        q = lax.rem(mine_a + d, n_a)
        return (zz * plane + q // 2, lax.rem(q, 2))

    def peer_b(d):
        return (lax.rem(zz + d, nz) * plane + in_plane, gen)

    nblk = buses // 256
    ptdf_copies = []
    for c in range(nblk):
        cp = pltpu.make_async_copy(
            ptdf_h.at[:, pl.ds(c * 256, 256)], ptdf.at[:, pl.ds(c * 256, 256)], ptdf_sem.at[c]
        )
        cp.start()
        ptdf_copies.append(cp)
    loads = [
        pltpu.make_async_copy(s, d, load_sem.at[i])
        for i, (s, d) in enumerate(
            [
                (y_h, yv), (mu_h, muv.at[pl.ds(0, rows)]), (x_h, xv), (base_h, basev), (cost_h, cost),
                (lo_h, lo), (hi_h, hi), (ramp_h, ramp), (pinit_h, pinit), (lim_h, lim), (dem_h, dem),
                (lam_h, lam),
            ]
        )
    ]
    for cp in loads:
        cp.start()

    barrier = pltpu.get_barrier_semaphore()

    def greet(dev):
        pl.semaphore_signal(barrier, inc=1, device_id=dev, device_id_type=MESH)

    greet(nxt)
    greet(prv)

    @pl.loop(1, n_a)
    def _(d):
        greet(peer_a(d))

    @pl.loop(1, nz)
    def _(d):
        greet(peer_b(d))

    nlb = lines // 128
    eye = (
        lax.broadcasted_iota(jnp.int32, (256, 256), 0)
        == lax.broadcasted_iota(jnp.int32, (256, 256), 1)
    ).astype(BF16)
    for c in range(nblk):
        ptdf_copies[c].wait()
        turned = lax.dot_general(
            eye, ptdf[:, c * 256 : (c + 1) * 256], (((1,), (1,)), ((), ())),
            preferred_element_type=F32,
        )
        for j in range(nlb):
            table[pl.ds(c * 256, 256), j, :] = turned[:, j * 128 : (j + 1) * 128]

    for cp in loads:
        cp.wait()
    yb[0, gen] = yv[...].astype(BF16)
    pl.semaphore_wait(barrier, n_a - 1 + nz - 1 + 2)

    def send_yb(it):
        return pltpu.make_async_remote_copy(
            yb.at[it, gen], yb.at[it, gen], yb_send.at[it], yb_recv.at[it],
            device_id=partner, device_id_type=MESH,
        )

    def send_row(k, src, dst, dev):
        return pltpu.make_async_remote_copy(
            src, dst, row_send.at[k], row_recv.at[k], device_id=dev, device_id_type=MESH
        )

    yb_copy = send_yb(0)
    yb_copy.start()
    mu_copy = send_row(0, muv.at[pl.ds(0, 1)], mu_next, prv)
    mu_copy.start()

    group = 16

    @pl.loop(0, gl // (2 * group))
    def _(i):
        for s in range(2):
            g0 = pl.multiple_of((i * 2 + s) * group, group)
            for k in range(group):
                stage[pl.ds((s * group + k) * nlb, nlb), :] = table[bus[g0 + k]]
            for j in range(nlb):
                got = stage[pl.ds(s * group * nlb + j, group, stride=nlb), :]
                fac[j // (nlb // 2), pl.ds(g0, group), pl.ds((j % (nlb // 2)) * 128, 128)] = got.astype(BF16)

    eye_r = lax.broadcasted_iota(jnp.int32, (rows, rows), 0) == lax.broadcasted_iota(
        jnp.int32, (rows, rows), 1
    )

    def to_column(row):
        return jnp.sum(jnp.where(eye_r, jnp.broadcast_to(row, (rows, rows)), 0.0), axis=1, keepdims=True)

    def to_row(col):
        return jnp.sum(jnp.where(eye_r, jnp.broadcast_to(col, (rows, rows)), 0.0), axis=0, keepdims=True)

    last = tm == ntm - 1
    first = tm == 0
    lam_col = to_column(lam[...])
    dem_col = to_column(dem[...])
    yb_copy.wait()
    mu_copy.wait()
    muv[pl.ds(rows, 1), :] = jnp.where(last, 0.0, mu_next[...])

    gc = 512
    sums = []
    outs = []
    for it in range(ITERS):
        acc_p[...] = jnp.zeros_like(acc_p)
        acc_d[...] = jnp.zeros_like(acc_d)
        acc_t[...] = jnp.zeros_like(acc_t)
        wlam = w * lam_col

        @pl.loop(0, gl // gc)
        def _(c):
            sl = pl.ds(pl.multiple_of(c * gc, gc), gc)
            pulled = lax.dot_general(
                yb[it, 0], fac[0, sl, :], (((1,), (1,)), ((), ())), preferred_element_type=F32
            ) + lax.dot_general(
                yb[it, 1], fac[1, sl, :], (((1,), (1,)), ((), ())), preferred_element_type=F32
            )
            xc = xv[:, sl]
            grad = cost[:, sl] + wlam + pulled + muv[pl.ds(0, rows), sl] - muv[pl.ds(1, rows), sl]
            xn = jnp.clip(xc - TAU * grad, lo[:, sl], hi[:, sl])
            xb = 2.0 * xn - xc
            d = xn - xc
            d2 = d * d
            xv[:, sl] = xn
            xbv[pl.ds(8, rows), sl] = xb
            xbb[:, sl] = xb.astype(BF16)
            acc_p[...] += sum(d2[:, k * 128 : (k + 1) * 128] for k in range(gc // 128))
            acc_t[...] += sum(xb[:, k * 128 : (k + 1) * 128] for k in range(gc // 128))

        rows_out = [send_row(1 + 2 * it, xbv.at[pl.ds(8 + rows - 1, 1)], xb_prev.at[it], nxt)]
        if it < ITERS - 1:
            rows_out.append(send_row(2 + 2 * it, xbv.at[pl.ds(8, 1)], xb_next, prv))
        for cp in rows_out:
            cp.start()
        if it == ITERS - 1:
            cp = pltpu.make_async_copy(xv, xo_h, out_sem.at[0])
            cp.start()
            outs.append(cp)

        tot_col = w * jnp.sum(acc_t[...], axis=1, keepdims=True)
        fsend[it, pl.ds(0, rows), :] = jnp.dot(xbb[...], fac[other], preferred_element_type=F32)
        fsend[it, pl.ds(rows, 1), pl.ds(0, rows)] = to_row(tot_col)
        f_copy = pltpu.make_async_remote_copy(
            fsend.at[it], frecv.at[it], f_send.at[it], f_recv.at[it],
            device_id=partner, device_id_type=MESH,
        )
        f_copy.start()
        flow_own[...] = jnp.dot(xbb[...], fac[gen], preferred_element_type=F32)

        for cp in rows_out:
            cp.wait()
        xbv[pl.ds(7, 1), :] = jnp.where(first, pinit[...], xb_prev[it])
        if it < ITERS - 1:
            m_n = muv[pl.ds(rows, 1), :]
            u_n = m_n + SIGMA * (xb_next[...] - xbv[pl.ds(8 + rows - 1, 1), :])
            mn_n = u_n - jnp.clip(u_n, -SIGMA * ramp[...], SIGMA * ramp[...])
            muv[pl.ds(rows, 1), :] = jnp.where(last, 0.0, mn_n)

        @pl.loop(0, gl // gc)
        def _(c):
            sl = pl.ds(pl.multiple_of(c * gc, gc), gc)
            m = muv[pl.ds(0, rows), sl]
            u = m + SIGMA * (xbv[pl.ds(8, rows), sl] - xbv[pl.ds(7, rows), sl])
            r = SIGMA * ramp[:, sl]
            mn = u - jnp.clip(u, -r, r)
            muv[pl.ds(0, rows), sl] = mn
            d = mn - m
            d2 = d * d
            acc_d[...] += sum(d2[:, k * 128 : (k + 1) * 128] for k in range(gc // 128))

        if it == ITERS - 1:
            cp = pltpu.make_async_copy(muv.at[pl.ds(0, rows)], muo_h, out_sem.at[1])
            cp.start()
            outs.append(cp)

        f_copy.wait()
        yo = yv[...]
        v = yo + SIGMA * (flow_own[...] + frecv[it, pl.ds(0, rows), :])
        bv = basev[...]
        lv = lim[...]
        yn = v - jnp.clip(v, SIGMA * (bv - lv), SIGMA * (bv + lv))
        yv[...] = yn
        if it < ITERS - 1:
            yb[it + 1, gen] = yn.astype(BF16)
            yb_copy = send_yb(it + 1)
            yb_copy.start()
        else:
            cp = pltpu.make_async_copy(yv, yo_h, out_sem.at[2])
            cp.start()
            outs.append(cp)
        dy = yn - yo
        dy2 = dy * dy
        acc_d[...] += sum(dy2[:, k * 128 : (k + 1) * 128] for k in range(half // 128))
        totals = tot_col + to_column(frecv[it, pl.ds(rows, 1), pl.ds(0, rows)])
        lam_new = lam_col + SIGMA * (totals - dem_col)
        dl = lam_new - lam_col
        lam_col = lam_new
        primal = jnp.sum(acc_p[...], keepdims=True) / (TAU * cells)
        dual = (
            jnp.sum(acc_d[...], keepdims=True)
            + jnp.where(gen == 0, jnp.sum(dl * dl, keepdims=True), 0.0)
        ) / (SIGMA * cells)
        sums += [primal, dual]
        if it < ITERS - 1:
            yb_copy.wait()

    lane = lax.broadcasted_iota(jnp.int32, (1, 128), 1)
    packed = jnp.zeros((1, 128), F32)
    for k, s in enumerate(sums):
        packed = jnp.where(lane == k, s, packed)

    def all_sum(value, buf, k, n, mine, peer):
        msg[k] = value
        buf[mine] = value

        @pl.loop(1, n)
        def _(d):
            pltpu.make_async_remote_copy(
                msg.at[k], buf.at[mine], ar_send.at[k], ar_recv.at[k],
                device_id=peer(d), device_id_type=MESH,
            ).start()

        several = buf.at[pl.ds(0, n - 1)]
        pltpu.make_async_copy(several, several, ar_send.at[k]).wait()
        pltpu.make_async_copy(several, several, ar_recv.at[k]).wait()
        return jnp.sum(buf[...], axis=0)

    total = all_sum(packed, ar_a, 0, n_a, mine_a, peer_a)
    total = all_sum(total, ar_b, 1, nz, zz, peer_b)
    place = 2 * lax.broadcasted_iota(jnp.int32, (ITERS, 2), 0) + lax.broadcasted_iota(
        jnp.int32, (ITERS, 2), 1
    )
    result = jnp.zeros((ITERS, 2), F32)
    for k in range(2 * ITERS):
        one = jnp.sum(jnp.where(lane == k, total, 0.0), axis=1, keepdims=True)
        result = jnp.where(place == k, one, result)
    mov_o[...] = result
    lam_o[...] = to_row(lam_col)
    for cp in outs:
        cp.wait()


def on_device(ntm, plane, hours, gl_total,
              dispatch, cost, p_low, p_high, ramp_limit, p_init, demand, bus_of, ptdf, line_base,
              line_limit, line_dual, ramp_dual, balance_dual):
    rows, gl = dispatch.shape
    lines, buses = ptdf.shape
    half = lines // 2
    n_a = 2 * plane
    nz = ntm // plane
    row = lambda a: a.reshape(1, -1)
    any_ = pl.BlockSpec(memory_space=pl.ANY)
    vmem = pl.BlockSpec(memory_space=pltpu.VMEM)
    smem = pl.BlockSpec(memory_space=pltpu.SMEM)
    V = pltpu.VMEM
    S = pltpu.SemaphoreType.DMA
    x, y, mu, lam, mov = pl.pallas_call(
        functools.partial(kernel, (ntm, plane, gl_total, hours)),
        name="dispatch_step",
        out_shape=(
            jax.ShapeDtypeStruct((rows, gl), F32),
            jax.ShapeDtypeStruct((rows, half), F32),
            jax.ShapeDtypeStruct((rows, gl), F32),
            jax.ShapeDtypeStruct((1, rows), F32),
            jax.ShapeDtypeStruct((ITERS, 2), F32),
        ),
        in_specs=[smem] + [any_] * 13,
        out_specs=(any_, any_, any_, vmem, vmem),
        scratch_shapes=[
            V((lines, buses), BF16),
            V((buses, lines // 128, 128), F32),
            V((32 * (lines // 128), 128), F32),
            V((2, gl, half), BF16),
            V((rows, gl), F32),
            V((rows + 8, gl), F32),
            V((rows + 8, gl), F32),
            V((rows, gl), BF16),
            V((rows, half), F32),
            V((rows, half), F32),
            V((rows, half), F32),
            V((ITERS, 2, rows, half), BF16),
            V((ITERS, rows + 8, half), F32),
            V((ITERS, rows + 8, half), F32),
            V((1, gl), F32), V((1, gl), F32), V((1, gl), F32), V((1, gl), F32), V((1, gl), F32),
            V((1, half), F32), V((1, rows), F32), V((1, rows), F32),
            V((1, gl), F32), V((ITERS, 1, gl), F32), V((1, gl), F32),
            V((rows, 128), F32), V((rows, 128), F32), V((rows, 128), F32),
            V((2, 1, 128), F32), V((n_a, 1, 128), F32), V((nz, 1, 128), F32),
            S((12,)), S((buses // 256,)), S((3,)), S((ITERS,)), S((ITERS,)), S((ITERS,)), S((ITERS,)),
            S((2 * ITERS,)), S((2 * ITERS,)), S((2,)), S((2,)),
        ],
        compiler_params=pltpu.CompilerParams(
            collective_id=0, has_side_effects=True, vmem_limit_bytes=48 * 1024 * 1024
        ),
    )(
        bus_of, dispatch, row(cost), row(p_low), row(p_high), row(ramp_limit), row(p_init), row(demand),
        ptdf, line_base, row(line_limit), line_dual, ramp_dual, row(balance_dual),
    )
    return x, y, mu, lam.reshape(-1), mov


def solution(mesh):
    ntm = mesh.shape["tm"]
    plane = min(PLANE, ntm)

    def body(*args):
        return on_device(ntm, plane, args[0].shape[0] * ntm, args[0].shape[1] * mesh.shape["gen"], *args)

    in_specs = (
        P("tm", "gen"), P("gen"), P("gen"), P("gen"), P("gen"), P("gen"), P("tm"), P("gen"), P(),
        P("tm", "gen"), P("gen"), P("tm", "gen"), P("tm", "gen"), P("tm"),
    )
    out_specs = (P("tm", "gen"), P("tm", "gen"), P("tm", "gen"), P("tm"), P())
    return jax.shard_map(body, mesh=mesh, in_specs=in_specs, out_specs=out_specs, check_vma=False)
```

time: 176 us -> 75 us (0.43)
  Pallas kernels: 0 us -> 60.1 us
  blocking collectives: 42.4 us -> 0 us
  starting transfers between devices: 30.4 us -> 0 us
  local copies, waits for them, and re-layouts: 43.1 us -> 13.6 us
  other arithmetic: 24.5 us -> 0 us
  matrix products: 18.3 us -> 0 us
  waiting for transfers between devices: 10.2 us -> 0 us
  between operations: 6.06 us -> 0.67 us
    pallas_call x0 -> x1, Pallas kernels: none -> 60.1 us  [on_device(): pl.pallas_call(functools.partial(kernel, (ntm, plane, gl_total, hours)),...]
    psum x5 -> x0, blocking collectives: 42.4 us -> none  [over_axes(): return functools.reduce(lax.psum, axes, array)]
    gather x1 -> x0, local copies, waits for them, and re-layouts: 23.6 us -> none  [on_device(): columns = jnp.take(ptdf, bus_of, axis=1)]
    dot_general x4 -> x0, matrix products: 18.3 us -> none  [the longest x2 15 us: on_device(): pulled = jnp.dot(rounded, columns, preferred_element_type=jnp.float32)]
    all_to_all x4 -> x0, starting transfers between devices: 18.2 us -> none  [sent_to_all(): lax.all_to_all(jnp.broadcast_to(array[None], (peers, *array.shape)), axis...]
    reduce_sum x5 -> x0, other arithmetic: 12.3 us -> none  [the longest x2 5.33 us: over_copies(): return jnp.sum(everything, axis=0)]
    ppermute x4 -> x0, starting transfers between devices: 12.2 us -> none  [passed_along(): return lax.ppermute(block, axis, route)]
    all_to_all x4 -> x0, waiting for transfers between devices: 10.2 us -> none  [sent_to_all(): lax.all_to_all(jnp.broadcast_to(array[None], (peers, *array.shape)), axis...]
  transfers between devices with their start and end apart: 8 -> 0, of which waited for: 2 -> 0; matrix products, arithmetic and copies ran while one was open for 33% -> 0% of each run, Pallas kernels for 0% -> 0%
where the time goes in v1:
time: 75 us; the launch traced here: 74.4 us
  Pallas kernels  60.1 us (80%)
  local copies, waits for them, and re-layouts  13.6 us (18%)
    pallas_call x1, Pallas kernels, on_device(): pl.pallas_call(functools.partial(kernel, (ntm, plane, gl_total, hours)),...  60.1 us
    unnamed x29, local copies, waits for them, and re-layouts  13.6 us

profile of v1, /device:TPU:1, one launch (start us, length us, event | category | flops | bytes accessed | tf_op | source)
XLA Modules:
  0.0 74.4 jit_solution(11492000381764142623)
XLA Ops:
  0.6 0.0 copy-start
  0.6 1.4 %copy-done = f32[96,4096]{1,0:T(8,128)S(1)} copy-done((f32[96,4096]{1,0:T(8,128)S(1)}, f32[96,4096]{1,0:T(8,128)}, u32[]{:S(2)}) %copy-start) | copy-done | bytes 1572888
  2.0 0.0 copy-start.1
  2.0 0.9 %copy-done.1 = f32[96,512]{1,0:T(8,128)S(1)} copy-done((f32[96,512]{1,0:T(8,128)S(1)}, f32[96,512]{1,0:T(8,128)}, u32[]{:S(2)}) %copy-start.1) | copy-done | bytes 196632
  3.0 0.0 copy-start.2
  3.0 0.9 %copy-done.2 = f32[96,512]{1,0:T(8,128)S(1)} copy-done((f32[96,512]{1,0:T(8,128)S(1)}, f32[96,512]{1,0:T(8,128)}, u32[]{:S(2)}) %copy-start.2) | copy-done | bytes 196632
  3.9 0.0 copy-start.3
  3.9 0.7 copy-done.3
  4.6 0.0 copy-start.4
  4.6 0.7 copy-done.4
  5.3 0.0 copy-start.5
  5.3 0.7 copy-done.5
  6.1 0.0 copy-start.6
  6.1 0.7 copy-done.6
  6.8 0.0 copy-start.7
  6.8 0.7 copy-done.7
  7.5 0.0 copy-start.8
  7.5 0.7 copy-done.8
  8.2 0.0 copy-start.9
  8.2 0.7 copy-done.9
  8.9 0.0 copy-start.10
  8.9 0.7 copy-done.10
  9.5 0.0 copy-start.11
  9.5 0.7 copy-done.11
  10.2 60.1 %dispatch_step.1 = (f32[96,4096]{1,0:T(8,128)S(1)}, f32[96,512]{1,0:T(8,128)S(1)}, f32[96,4096]{1,0:T(8,128)S(1)}, f32[1,96]{1,0:T(1,128)S(1)}, f32[2,2]{1,0:T(2,128)S(1)}) custom-call(s32[4096]{0:T(1024)S(1)} %copy-done.3, f32[96,4096]{1,0:T(8,128)S(1)} %copy-done, f32[1,4096]{1,0:T(1,128)S(1)} %bitcast.9, f32[1,4096]{1,0:T(1,128)S(1)} %bitcast.10, ...), custom_call_target="tpu_custom_call" | custom-call | tf_op jit(solution)/shard_map/dispatch_step/pallas_call | solution.py:312
  70.3 1.1 %copy.24 = f32[96,4096]{1,0:T(8,128)} copy(f32[96,4096]{1,0:T(8,128)S(1)} %get-tuple-element.20) | data formatting | bytes 3145728
  71.5 0.7 copy.25
  72.1 1.1 %copy.26 = f32[96,4096]{1,0:T(8,128)} copy(f32[96,4096]{1,0:T(8,128)S(1)} %get-tuple-element.22) | data formatting | bytes 3145728
  73.3 0.5 copy.27
  73.8 0.6 copy.28
Async XLA Ops:
  0.6 1.4 %copy-start = (f32[96,4096]{1,0:T(8,128)S(1)}, f32[96,4096]{1,0:T(8,128)}, u32[]{:S(2)}) copy-start(f32[96,4096]{1,0:T(8,128)} %x_h.1) | copy-start | bytes 4718596
  2.0 0.9 %copy-start.1 = (f32[96,512]{1,0:T(8,128)S(1)}, f32[96,512]{1,0:T(8,128)}, u32[]{:S(2)}) copy-start(f32[96,512]{1,0:T(8,128)} %base_h.1) | copy-start | bytes 589828
  3.0 0.9 %copy-start.2 = (f32[96,512]{1,0:T(8,128)S(1)}, f32[96,512]{1,0:T(8,128)}, u32[]{:S(2)}) copy-start(f32[96,512]{1,0:T(8,128)} %y_h.1) | copy-start | bytes 589828
  3.9 0.7 copy-start.3
  4.6 0.7 copy-start.4
  5.3 0.7 copy-start.5
  6.1 0.7 copy-start.6
  6.8 0.7 copy-start.7
  7.5 0.7 copy-start.8
  8.2 0.7 copy-start.9
  8.9 0.7 copy-start.10
  9.5 0.7 copy-start.11

commit v2 on v1

--- a/solution.py
+++ b/solution.py
@@ -19,10 +19,10 @@
 
 def kernel(
     cfg,
-    bus, x_h, cost_h, lo_h, hi_h, ramp_h, pinit_h, dem_h, ptdf_h, base_h, lim_h, y_h, mu_h, lam_h,
+    bus_h, x_h, cost_h, lo_h, hi_h, ramp_h, pinit_h, dem_h, ptdf_h, base_h, lim_h, y_h, mu_h, lam_h,
     xo_h, yo_h, muo_h, lam_o, mov_o,
     ptdf, table, stage, fac, xv, muv, xbv, xbb, yv, basev, flow_own, yb, fsend, frecv,
-    cost, lo, hi, ramp, pinit, lim, dem, lam, mu_next, xb_prev, xb_next,
+    bus, cost, lo, hi, ramp, pinit, lim, dem, lam, mu_next, xb_prev, xb_next,
     acc_p, acc_d, acc_t, msg, ar_a, ar_b,
     load_sem, ptdf_sem, out_sem, yb_send, yb_recv, f_send, f_recv, row_send, row_recv, ar_send, ar_recv,
 ):
@@ -52,11 +52,11 @@
         return (lax.rem(zz + d, nz) * plane + in_plane, gen)
 
     nblk = buses // 256
+    per_load = nblk // 2
     ptdf_copies = []
-    for c in range(nblk):
-        cp = pltpu.make_async_copy(
-            ptdf_h.at[:, pl.ds(c * 256, 256)], ptdf.at[:, pl.ds(c * 256, 256)], ptdf_sem.at[c]
-        )
+    for c in range(2):
+        part = pl.ds(c * per_load * 256, per_load * 256)
+        cp = pltpu.make_async_copy(ptdf_h.at[:, part], ptdf.at[:, part], ptdf_sem.at[c])
         cp.start()
         ptdf_copies.append(cp)
     loads = [
@@ -65,7 +65,7 @@
             [
                 (y_h, yv), (mu_h, muv.at[pl.ds(0, rows)]), (x_h, xv), (base_h, basev), (cost_h, cost),
                 (lo_h, lo), (hi_h, hi), (ramp_h, ramp), (pinit_h, pinit), (lim_h, lim), (dem_h, dem),
-                (lam_h, lam),
+                (lam_h, lam), (bus_h, bus),
             ]
         )
     ]
@@ -89,18 +89,20 @@
         greet(peer_b(d))
 
     nlb = lines // 128
+    flat = table.reshape(buses * nlb, 128)
     eye = (
         lax.broadcasted_iota(jnp.int32, (256, 256), 0)
         == lax.broadcasted_iota(jnp.int32, (256, 256), 1)
     ).astype(BF16)
     for c in range(nblk):
-        ptdf_copies[c].wait()
+        if c % per_load == 0:
+            ptdf_copies[c // per_load].wait()
         turned = lax.dot_general(
             eye, ptdf[:, c * 256 : (c + 1) * 256], (((1,), (1,)), ((), ())),
             preferred_element_type=F32,
         )
         for j in range(nlb):
-            table[pl.ds(c * 256, 256), j, :] = turned[:, j * 128 : (j + 1) * 128]
+            flat[pl.ds(c * 256 * nlb + j, 256, stride=nlb), :] = turned[:, j * 128 : (j + 1) * 128]
 
     for cp in loads:
         cp.wait()
@@ -124,16 +126,27 @@
     mu_copy.start()
 
     group = 16
-
-    @pl.loop(0, gl // (2 * group))
+    n_group = 128 // group
+
+    @pl.loop(0, gl // 128)
     def _(i):
-        for s in range(2):
-            g0 = pl.multiple_of((i * 2 + s) * group, group)
-            for k in range(group):
-                stage[pl.ds((s * group + k) * nlb, nlb), :] = table[bus[g0 + k]]
+        def fetch(s, k):
+            stage[pl.ds((s * group + k) * nlb, nlb), :] = table[bus[i, s * group + k]]
+
+        def pack(s, j):
+            g0 = pl.multiple_of(i * 128 + s * group, group)
+            got = stage[pl.ds(s * group * nlb + j, group, stride=nlb), :]
+            fac[j // (nlb // 2), pl.ds(g0, group), pl.ds((j % (nlb // 2)) * 128, 128)] = got.astype(BF16)
+
+        for k in range(group):
+            fetch(0, k)
+        for s in range(n_group):
+            per = group // nlb
             for j in range(nlb):
-                got = stage[pl.ds(s * group * nlb + j, group, stride=nlb), :]
-                fac[j // (nlb // 2), pl.ds(g0, group), pl.ds((j % (nlb // 2)) * 128, 128)] = got.astype(BF16)
+                if s + 1 < n_group:
+                    for k in range(per):
+                        fetch(s + 1, j * per + k)
+                pack(s, j)
 
     eye_r = lax.broadcasted_iota(jnp.int32, (rows, rows), 0) == lax.broadcasted_iota(
         jnp.int32, (rows, rows), 1
@@ -304,9 +317,8 @@
     n_a = 2 * plane
     nz = ntm // plane
     row = lambda a: a.reshape(1, -1)
-    any_ = pl.BlockSpec(memory_space=pl.ANY)
+    any_ = pl.BlockSpec(memory_space=pltpu.HBM)
     vmem = pl.BlockSpec(memory_space=pltpu.VMEM)
-    smem = pl.BlockSpec(memory_space=pltpu.SMEM)
     V = pltpu.VMEM
     S = pltpu.SemaphoreType.DMA
     x, y, mu, lam, mov = pl.pallas_call(
@@ -319,12 +331,12 @@
             jax.ShapeDtypeStruct((1, rows), F32),
             jax.ShapeDtypeStruct((ITERS, 2), F32),
         ),
-        in_specs=[smem] + [any_] * 13,
+        in_specs=[any_] * 14,
         out_specs=(any_, any_, any_, vmem, vmem),
         scratch_shapes=[
             V((lines, buses), BF16),
             V((buses, lines // 128, 128), F32),
-            V((32 * (lines // 128), 128), F32),
+            V((128 * (lines // 128), 128), F32),
             V((2, gl, half), BF16),
             V((rows, gl), F32),
             V((rows + 8, gl), F32),
@@ -336,19 +348,20 @@
             V((ITERS, 2, rows, half), BF16),
             V((ITERS, rows + 8, half), F32),
             V((ITERS, rows + 8, half), F32),
+            pltpu.SMEM((gl // 128, 128), jnp.int32),
             V((1, gl), F32), V((1, gl), F32), V((1, gl), F32), V((1, gl), F32), V((1, gl), F32),
             V((1, half), F32), V((1, rows), F32), V((1, rows), F32),
             V((1, gl), F32), V((ITERS, 1, gl), F32), V((1, gl), F32),
             V((rows, 128), F32), V((rows, 128), F32), V((rows, 128), F32),
             V((2, 1, 128), F32), V((n_a, 1, 128), F32), V((nz, 1, 128), F32),
-            S((12,)), S((buses // 256,)), S((3,)), S((ITERS,)), S((ITERS,)), S((ITERS,)), S((ITERS,)),
+            S((13,)), S((2,)), S((3,)), S((ITERS,)), S((ITERS,)), S((ITERS,)), S((ITERS,)),
             S((2 * ITERS,)), S((2 * ITERS,)), S((2,)), S((2,)),
         ],
         compiler_params=pltpu.CompilerParams(
-            collective_id=0, has_side_effects=True, vmem_limit_bytes=48 * 1024 * 1024
+            collective_id=0, has_side_effects=True, vmem_limit_bytes=60 * 1024 * 1024
         ),
     )(
-        bus_of, dispatch, row(cost), row(p_low), row(p_high), row(ramp_limit), row(p_init), row(demand),
+        bus_of.reshape(-1, 128), dispatch, row(cost), row(p_low), row(p_high), row(ramp_limit), row(p_init), row(demand),
         ptdf, line_base, row(line_limit), line_dual, ramp_dual, row(balance_dual),
     )
     return x, y, mu, lam.reshape(-1), mov

time: 75 us -> 62.6 us (0.83)
  local copies, waits for them, and re-layouts: 13.6 us -> 5.69 us
  Pallas kernels: 60.1 us -> 56.2 us
    unnamed x29 -> x13, local copies, waits for them, and re-layouts: 13.6 us -> 5.69 us
    pallas_call x1, Pallas kernels: 60.1 us -> 56.2 us  [on_device(): pl.pallas_call(functools.partial(kernel, (ntm, plane, gl_total, hours)),...]
where the time goes in v2:
time: 62.6 us
  Pallas kernels  56.2 us (90%)
  local copies, waits for them, and re-layouts  5.69 us (9%)
  between operations  0.67 us (1%)
    pallas_call x1, Pallas kernels, on_device(): pl.pallas_call(functools.partial(kernel, (ntm, plane, gl_total, hours)),...  56.2 us
    unnamed x13, local copies, waits for them, and re-layouts  5.69 us

profile of v2, /device:TPU:1, one launch (start us, length us, event | category | flops | bytes accessed | tf_op | source)
XLA Modules:
  0.0 62.6 jit_solution(16401967216187809601)
XLA Ops:
  0.6 56.2 %dispatch_step.1 = (f32[96,4096]{1,0:T(8,128)}, f32[96,512]{1,0:T(8,128)}, f32[96,4096]{1,0:T(8,128)}, f32[1,96]{1,0:T(1,128)}, f32[2,2]{1,0:T(2,128)}) custom-call(s32[32,128]{1,0:T(8,128)} %bitcast.10, f32[96,4096]{1,0:T(8,128)} %x_h.1, f32[1,4096]{1,0:T(1,128)} %bitcast.11, f32[1,4096]{1,0:T(1,128)} %bitcast.12, f32[1,4096]{1,0:T(1,128)} %bitcast.13, ...), custom_call_target="tpu_custom_call" | custom-call | tf_op jit(solution)/shard_map/dispatch_step/pallas_call | solution.py:324
  56.8 0.0 copy-start.1
  56.9 0.0 copy-start
  56.9 2.8 %copy.24 = f32[96,4096]{1,0:T(8,128)} copy(f32[96,4096]{1,0:T(8,128)} %get-tuple-element.20) | data formatting | bytes 3145728
  59.6 0.0 copy-done.1
  59.6 0.7 %copy.25 = f32[96,512]{1,0:T(8,128)} copy(f32[96,512]{1,0:T(8,128)S(1)} %copy-done.1) | data formatting | bytes 393216
  60.3 0.0 copy-done
  60.3 0.0 copy-start.3
  60.3 0.0 copy-start.2
  60.3 1.1 %copy.26 = f32[96,4096]{1,0:T(8,128)} copy(f32[96,4096]{1,0:T(8,128)S(1)} %copy-done) | data formatting | bytes 3145728
  61.5 0.0 copy-done.3
  61.5 0.5 copy.27
  62.0 0.0 copy-done.2
  62.0 0.6 copy.28
Async XLA Ops:
  56.8 2.8 %copy-start.1 = (f32[96,512]{1,0:T(8,128)S(1)}, f32[96,512]{1,0:T(8,128)}, u32[]{:S(2)}) copy-start(f32[96,512]{1,0:T(8,128)} %get-tuple-element.21) | copy-start | bytes 589828
  56.9 3.5 %copy-start = (f32[96,4096]{1,0:T(8,128)S(1)}, f32[96,4096]{1,0:T(8,128)}, u32[]{:S(2)}) copy-start(f32[96,4096]{1,0:T(8,128)} %get-tuple-element.22) | copy-start | bytes 4718596
  60.3 1.1 %copy-start.3 = (f32[1,96]{1,0:T(1,128)S(1)}, f32[1,96]{1,0:T(1,128)}, u32[]{:S(2)}) copy-start(f32[1,96]{1,0:T(1,128)} %get-tuple-element.13) | copy-start | bytes 1156
  60.3 1.7 %copy-start.2 = (f32[2,2]{1,0:T(2,128)S(1)}, f32[2,2]{1,0:T(2,128)}, u32[]{:S(2)}) copy-start(f32[2,2]{1,0:T(2,128)} %get-tuple-element.24) | copy-start | bytes 52

commit v3 on v2

--- a/solution.py
+++ b/solution.py
@@ -20,11 +20,12 @@
 def kernel(
     cfg,
     bus_h, x_h, cost_h, lo_h, hi_h, ramp_h, pinit_h, dem_h, ptdf_h, base_h, lim_h, y_h, mu_h, lam_h,
-    xo_h, yo_h, muo_h, lam_o, mov_o,
-    ptdf, table, stage, fac, xv, muv, xbv, xbb, yv, basev, flow_own, yb, fsend, frecv,
-    bus, cost, lo, hi, ramp, pinit, lim, dem, lam, mu_next, xb_prev, xb_next,
+    xv, yo, muo, lam_o, mov_o,
+    ptdf, table, stage, fac, muv, xbv, xbb, yv, yt, bt, flow, yb, ybs, frecv,
+    bus, cost, lo, hi, ramp, pinit, lim, lim_x, dem, lam, mu_next, xb_prev, xb_next, tot, tot_x,
     acc_p, acc_d, acc_t, msg, ar_a, ar_b,
-    load_sem, ptdf_sem, out_sem, yb_send, yb_recv, f_send, f_recv, row_send, row_recv, ar_send, ar_recv,
+    load_sem, ptdf_sem, yb_send, yb_recv, init_send, init_recv, f_send, f_recv, t_send, t_recv,
+    ys_send, ys_recv, yr_send, yr_recv, row_send, row_recv, ar_send, ar_recv,
 ):
     ntm, plane, gl_total, hours = cfg
     rows, gl = x_h.shape
@@ -39,6 +40,9 @@
     partner = (tm, other)
     nxt = (lax.rem(tm + 1, ntm), gen)
     prv = (lax.rem(tm + ntm - 1, ntm), gen)
+    twin = tm + 2 - 4 * lax.rem(tm // 2, 2)
+    top = pl.ds(0, rows // 2)
+    low = pl.ds(rows // 2, rows // 2)
     zz = tm // plane
     in_plane = lax.rem(tm, plane)
     n_a = 2 * plane
@@ -63,7 +67,7 @@
         pltpu.make_async_copy(s, d, load_sem.at[i])
         for i, (s, d) in enumerate(
             [
-                (y_h, yv), (mu_h, muv.at[pl.ds(0, rows)]), (x_h, xv), (base_h, basev), (cost_h, cost),
+                (y_h, yv), (mu_h, muv.at[pl.ds(0, rows)]), (x_h, xv), (cost_h, cost),
                 (lo_h, lo), (hi_h, hi), (ramp_h, ramp), (pinit_h, pinit), (lim_h, lim), (dem_h, dem),
                 (lam_h, lam), (bus_h, bus),
             ]
@@ -79,6 +83,8 @@
 
     greet(nxt)
     greet(prv)
+    greet((twin, 0))
+    greet((twin, 1))
 
     @pl.loop(1, n_a)
     def _(d):
@@ -107,12 +113,11 @@
     for cp in loads:
         cp.wait()
     yb[0, gen] = yv[...].astype(BF16)
-    pl.semaphore_wait(barrier, n_a - 1 + nz - 1 + 2)
-
-    def send_yb(it):
+    pl.semaphore_wait(barrier, n_a - 1 + nz - 1 + 4)
+
+    def send(src, dst, ssem, rsem, dev):
         return pltpu.make_async_remote_copy(
-            yb.at[it, gen], yb.at[it, gen], yb_send.at[it], yb_recv.at[it],
-            device_id=partner, device_id_type=MESH,
+            src, dst, ssem, rsem, device_id=dev, device_id_type=MESH
         )
 
     def send_row(k, src, dst, dev):
@@ -120,10 +125,19 @@
             src, dst, row_send.at[k], row_recv.at[k], device_id=dev, device_id_type=MESH
         )
 
-    yb_copy = send_yb(0)
+    yb_copy = send(yb.at[0, gen], yb.at[0, gen], yb_send, yb_recv, partner)
     yb_copy.start()
     mu_copy = send_row(0, muv.at[pl.ds(0, 1)], mu_next, prv)
     mu_copy.start()
+    moves = [
+        send(src.at[part], dst.at[part], init_send.at[i], init_recv.at[i], (twin, dev))
+        for i, (src, dst, part, dev) in enumerate(
+            [(y_h, yt, top, gen), (y_h, yt, low, other), (base_h, bt, top, gen), (base_h, bt, low, other)]
+        )
+    ]
+    moves.append(send(lim_h, lim_x, init_send.at[4], init_recv.at[4], (twin, other)))
+    for cp in moves:
+        cp.start()
 
     group = 16
     n_group = 128 // group
@@ -168,7 +182,6 @@
 
     gc = 512
     sums = []
-    outs = []
     for it in range(ITERS):
         acc_p[...] = jnp.zeros_like(acc_p)
         acc_d[...] = jnp.zeros_like(acc_d)
@@ -200,20 +213,20 @@
             rows_out.append(send_row(2 + 2 * it, xbv.at[pl.ds(8, 1)], xb_next, prv))
         for cp in rows_out:
             cp.start()
-        if it == ITERS - 1:
-            cp = pltpu.make_async_copy(xv, xo_h, out_sem.at[0])
-            cp.start()
-            outs.append(cp)
-
         tot_col = w * jnp.sum(acc_t[...], axis=1, keepdims=True)
-        fsend[it, pl.ds(0, rows), :] = jnp.dot(xbb[...], fac[other], preferred_element_type=F32)
-        fsend[it, pl.ds(rows, 1), pl.ds(0, rows)] = to_row(tot_col)
-        f_copy = pltpu.make_async_remote_copy(
-            fsend.at[it], frecv.at[it], f_send.at[it], f_recv.at[it],
-            device_id=partner, device_id_type=MESH,
-        )
-        f_copy.start()
-        flow_own[...] = jnp.dot(xbb[...], fac[gen], preferred_element_type=F32)
+        f_copies = []
+        for p in range(2):
+            flow[it, p] = jnp.dot(xbb[...], fac[p], preferred_element_type=F32)
+            for r, part in enumerate((top, low)):
+                cp = send(
+                    flow.at[it, p, part], frecv.at[it, gen, part], f_send.at[it, p * 2 + r],
+                    f_recv.at[it, gen * 2 + r], (twin, p if r == 0 else 1 - p),
+                )
+                cp.start()
+                f_copies.append(cp)
+        tot[it, :, pl.ds(0, rows)] = to_row(tot_col)
+        t_copy = send(tot.at[it], tot_x.at[it], t_send.at[it], t_recv.at[it], partner)
+        t_copy.start()
 
         for cp in rows_out:
             cp.wait()
@@ -231,38 +244,51 @@
             u = m + SIGMA * (xbv[pl.ds(8, rows), sl] - xbv[pl.ds(7, rows), sl])
             r = SIGMA * ramp[:, sl]
             mn = u - jnp.clip(u, -r, r)
-            muv[pl.ds(0, rows), sl] = mn
+            if it < ITERS - 1:
+                muv[pl.ds(0, rows), sl] = mn
+            else:
+                muo[:, sl] = mn
             d = mn - m
             d2 = d * d
             acc_d[...] += sum(d2[:, k * 128 : (k + 1) * 128] for k in range(gc // 128))
 
-        if it == ITERS - 1:
-            cp = pltpu.make_async_copy(muv.at[pl.ds(0, rows)], muo_h, out_sem.at[1])
-            cp.start()
-            outs.append(cp)
-
-        f_copy.wait()
-        yo = yv[...]
-        v = yo + SIGMA * (flow_own[...] + frecv[it, pl.ds(0, rows), :])
-        bv = basev[...]
-        lv = lim[...]
-        yn = v - jnp.clip(v, SIGMA * (bv - lv), SIGMA * (bv + lv))
-        yv[...] = yn
-        if it < ITERS - 1:
-            yb[it + 1, gen] = yn.astype(BF16)
-            yb_copy = send_yb(it + 1)
-            yb_copy.start()
-        else:
-            cp = pltpu.make_async_copy(yv, yo_h, out_sem.at[2])
-            cp.start()
-            outs.append(cp)
-        dy = yn - yo
-        dy2 = dy * dy
-        acc_d[...] += sum(dy2[:, k * 128 : (k + 1) * 128] for k in range(half // 128))
-        totals = tot_col + to_column(frecv[it, pl.ds(rows, 1), pl.ds(0, rows)])
+        t_copy.wait()
+        totals = tot_col + to_column(tot_x[it, :, pl.ds(0, rows)])
         lam_new = lam_col + SIGMA * (totals - dem_col)
         dl = lam_new - lam_col
         lam_col = lam_new
+
+        for cp in f_copies:
+            cp.wait_send()
+        for s in range(2):
+            for r, part in enumerate((top, low)):
+                send(
+                    flow.at[it, 0, part], frecv.at[it, s, part], f_send.at[it, r],
+                    f_recv.at[it, s * 2 + r], (twin, s),
+                ).wait_recv()
+        if it == 0:
+            for cp in moves:
+                cp.wait()
+        half_rows = rows // 2
+        for r, part in enumerate((top, low)):
+            old = yt[part, :]
+            v = old + SIGMA * (frecv[it, 0, part, :] + frecv[it, 1, part, :])
+            bv = bt[part, :]
+            lv = (lim if r == 0 else lim_x)[...]
+            yn = v - jnp.clip(v, SIGMA * (bv - lv), SIGMA * (bv + lv))
+            yt[part, :] = yn
+            if it < ITERS - 1:
+                ybs[part, :] = yn.astype(BF16)
+                for dev in range(2):
+                    send(
+                        ybs.at[part], yb.at[it + 1, gen if r == 0 else other, part],
+                        ys_send.at[dev * 2 + r], ys_recv.at[gen * 2 + r], (twin, dev),
+                    ).start()
+            dy = yn - old
+            dy2 = dy * dy
+            acc_d[pl.ds(r * half_rows, half_rows), :] += sum(
+                dy2[:, k * 128 : (k + 1) * 128] for k in range(half // 128)
+            )
         primal = jnp.sum(acc_p[...], keepdims=True) / (TAU * cells)
         dual = (
             jnp.sum(acc_d[...], keepdims=True)
@@ -270,14 +296,20 @@
         ) / (SIGMA * cells)
         sums += [primal, dual]
         if it < ITERS - 1:
-            yb_copy.wait()
+            for s in range(2):
+                for r, part in enumerate((top, low)):
+                    piece = s if r == 0 else 1 - s
+                    send(
+                        ybs.at[part], yb.at[it + 1, piece, part], ys_send.at[s * 2 + r],
+                        ys_recv.at[s * 2 + r], (twin, s),
+                    ).wait()
 
     lane = lax.broadcasted_iota(jnp.int32, (1, 128), 1)
     packed = jnp.zeros((1, 128), F32)
     for k, s in enumerate(sums):
         packed = jnp.where(lane == k, s, packed)
 
-    def all_sum(value, buf, k, n, mine, peer):
+    def all_sum(value, buf, k, n, mine, peer, between=None):
         msg[k] = value
         buf[mine] = value
 
@@ -288,12 +320,23 @@
                 device_id=peer(d), device_id_type=MESH,
             ).start()
 
+        if between is not None:
+            between()
         several = buf.at[pl.ds(0, n - 1)]
         pltpu.make_async_copy(several, several, ar_send.at[k]).wait()
         pltpu.make_async_copy(several, several, ar_recv.at[k]).wait()
         return jnp.sum(buf[...], axis=0)
 
-    total = all_sum(packed, ar_a, 0, n_a, mine_a, peer_a)
+    y_back = [
+        send(yt.at[part], yo.at[part], yr_send.at[r], yr_recv.at[r], (twin, dev))
+        for r, (part, dev) in enumerate(((top, gen), (low, other)))
+    ]
+
+    def return_y():
+        for cp in y_back:
+            cp.start()
+
+    total = all_sum(packed, ar_a, 0, n_a, mine_a, peer_a, return_y)
     total = all_sum(total, ar_b, 1, nz, zz, peer_b)
     place = 2 * lax.broadcasted_iota(jnp.int32, (ITERS, 2), 0) + lax.broadcasted_iota(
         jnp.int32, (ITERS, 2), 1
@@ -304,7 +347,18 @@
         result = jnp.where(place == k, one, result)
     mov_o[...] = result
     lam_o[...] = to_row(lam_col)
-    for cp in outs:
+    for cp in y_back:
+        cp.wait()
+
+
+def write_out(x, y, mu, lam, mov, x_h, y_h, mu_h, lam_h, mov_h, sem):
+    copies = [
+        pltpu.make_async_copy(s, d, sem.at[i])
+        for i, (s, d) in enumerate(((x, x_h), (mu, mu_h), (y, y_h), (lam, lam_h), (mov, mov_h)))
+    ]
+    for cp in copies:
+        cp.start()
+    for cp in copies:
         cp.wait()
 
 
@@ -317,53 +371,58 @@
     n_a = 2 * plane
     nz = ntm // plane
     row = lambda a: a.reshape(1, -1)
-    any_ = pl.BlockSpec(memory_space=pltpu.HBM)
+    hbm = pl.BlockSpec(memory_space=pltpu.HBM)
     vmem = pl.BlockSpec(memory_space=pltpu.VMEM)
     V = pltpu.VMEM
     S = pltpu.SemaphoreType.DMA
-    x, y, mu, lam, mov = pl.pallas_call(
+    shapes = ((rows, gl), (rows, half), (rows, gl), (1, rows), (ITERS, 2))
+    args = (
+        bus_of.reshape(-1, 128), dispatch, row(cost), row(p_low), row(p_high), row(ramp_limit), row(p_init),
+        row(demand), ptdf, line_base, row(line_limit), line_dual, ramp_dual, row(balance_dual),
+    )
+    state = pl.pallas_call(
         functools.partial(kernel, (ntm, plane, gl_total, hours)),
         name="dispatch_step",
-        out_shape=(
-            jax.ShapeDtypeStruct((rows, gl), F32),
-            jax.ShapeDtypeStruct((rows, half), F32),
-            jax.ShapeDtypeStruct((rows, gl), F32),
-            jax.ShapeDtypeStruct((1, rows), F32),
-            jax.ShapeDtypeStruct((ITERS, 2), F32),
-        ),
-        in_specs=[any_] * 14,
-        out_specs=(any_, any_, any_, vmem, vmem),
+        out_shape=tuple(V(shape, F32) for shape in shapes),
+        in_specs=[hbm] * len(args),
+        out_specs=(vmem,) * len(shapes),
         scratch_shapes=[
             V((lines, buses), BF16),
             V((buses, lines // 128, 128), F32),
             V((128 * (lines // 128), 128), F32),
             V((2, gl, half), BF16),
-            V((rows, gl), F32),
             V((rows + 8, gl), F32),
             V((rows + 8, gl), F32),
             V((rows, gl), BF16),
             V((rows, half), F32),
             V((rows, half), F32),
             V((rows, half), F32),
+            V((ITERS, 2, rows, half), F32),
             V((ITERS, 2, rows, half), BF16),
-            V((ITERS, rows + 8, half), F32),
-            V((ITERS, rows + 8, half), F32),
+            V((rows, half), BF16),
+            V((ITERS, 2, rows, half), F32),
             pltpu.SMEM((gl // 128, 128), jnp.int32),
             V((1, gl), F32), V((1, gl), F32), V((1, gl), F32), V((1, gl), F32), V((1, gl), F32),
-            V((1, half), F32), V((1, rows), F32), V((1, rows), F32),
-            V((1, gl), F32), V((ITERS, 1, gl), F32), V((1, gl), F32),
+            V((1, half), F32), V((1, half), F32), V((1, rows), F32), V((1, rows), F32),
+            V((1, gl), F32), V((ITERS, 1, gl), F32), V((1, gl), F32), V((ITERS, 1, 128), F32), V((ITERS, 1, 128), F32),
             V((rows, 128), F32), V((rows, 128), F32), V((rows, 128), F32),
             V((2, 1, 128), F32), V((n_a, 1, 128), F32), V((nz, 1, 128), F32),
-            S((13,)), S((2,)), S((3,)), S((ITERS,)), S((ITERS,)), S((ITERS,)), S((ITERS,)),
-            S((2 * ITERS,)), S((2 * ITERS,)), S((2,)), S((2,)),
+            S((12,)), S((2,)), S, S, S((5,)), S((5,)), S((ITERS, 4)), S((ITERS, 4)), S((ITERS,)), S((ITERS,)),
+            S((4,)), S((4,)), S((2,)), S((2,)), S((2 * ITERS,)), S((2 * ITERS,)), S((2,)), S((2,)),
         ],
         compiler_params=pltpu.CompilerParams(
-            collective_id=0, has_side_effects=True, vmem_limit_bytes=60 * 1024 * 1024
+            collective_id=0, has_side_effects=True, vmem_limit_bytes=48 * 1024 * 1024
         ),
-    )(
-        bus_of.reshape(-1, 128), dispatch, row(cost), row(p_low), row(p_high), row(ramp_limit), row(p_init), row(demand),
-        ptdf, line_base, row(line_limit), line_dual, ramp_dual, row(balance_dual),
-    )
+    )(*(pltpu.with_memory_space_constraint(a, pltpu.HBM) for a in args))
+    x, y, mu, lam, mov = pl.pallas_call(
+        write_out,
+        name="write_out",
+        out_shape=tuple(jax.ShapeDtypeStruct(shape, F32) for shape in shapes),
+        in_specs=[vmem] * len(shapes),
+        out_specs=(hbm,) * len(shapes),
+        scratch_shapes=[S((len(shapes),))],
+        compiler_params=pltpu.CompilerParams(vmem_limit_bytes=1024 * 1024),
+    )(*(pltpu.with_memory_space_constraint(a, pltpu.VMEM) for a in state))
     return x, y, mu, lam.reshape(-1), mov
 
 

time: 62.6 us -> 57.9 us (0.925)
  local copies, waits for them, and re-layouts: 5.69 us -> 0 us
  Pallas kernels: 56.2 us -> 57.2 us
    unnamed x13 -> x0, local copies, waits for them, and re-layouts: 5.69 us -> none
    pallas_call x0 -> x1, Pallas kernels: none -> 1.76 us  [on_device(): pl.pallas_call(write_out, name='write_out', out_shape=tuple((jax.ShapeDty...]
    pallas_call x1, Pallas kernels: 56.2 us -> 55.4 us  [on_device(): pl.pallas_call(functools.partial(kernel, (ntm, plane, gl_total, hours)),...]
where the time goes in v3:
time: 57.9 us; the launch traced here: 57.8 us
  Pallas kernels  57.2 us (99%)
  between operations  0.65 us (1%)
    pallas_call x1, Pallas kernels, on_device(): pl.pallas_call(functools.partial(kernel, (ntm, plane, gl_total, hours)),...  55.4 us
    pallas_call x1, Pallas kernels, on_device(): pl.pallas_call(write_out, name='write_out', out_shape=tuple((jax.ShapeDty...  1.76 us

profile of v3, /device:TPU:1, one launch (start us, length us, event | category | flops | bytes accessed | tf_op | source)
XLA Modules:
  0.0 57.8 jit_solution(640661235088937383)
XLA Ops:
  0.6 55.4 %dispatch_step.1 = (f32[96,4096]{1,0:T(8,128)S(1)}, f32[96,512]{1,0:T(8,128)S(1)}, f32[96,4096]{1,0:T(8,128)S(1)}, f32[1,96]{1,0:T(1,128)S(1)}, f32[2,2]{1,0:T(2,128)S(1)}) custom-call(s32[32,128]{1,0:T(8,128)} %bitcast.10, f32[96,4096]{1,0:T(8,128)} %x_h.1, f32[1,4096]{1,0:T(1,128)} %bitcast.11, f32[1,4096]{1,0:T(1,128)} %bitcast.12, f32[1,4096]{1,0:T(1,128)} %bitcast.13, ...), custom_call_target="tpu_custom_call" | custom-call | tf_op jit(solution)/shard_map/dispatch_step/pallas_call | solution.py:383
  56.1 1.8 %write_out.1 = (f32[96,4096]{1,0:T(8,128)}, f32[96,512]{1,0:T(8,128)}, f32[96,4096]{1,0:T(8,128)}, f32[1,96]{1,0:T(1,128)}, f32[2,2]{1,0:T(2,128)}) custom-call(f32[96,4096]{1,0:T(8,128)S(1)} %get-tuple-element.15.x, f32[96,512]{1,0:T(8,128)S(1)} %get-tuple-element.16.y, f32[96,4096]{1,0:T(8,128)S(1)} %get-tuple-element.17.mu, ...), custom_call_target="tpu_custom_call" | custom-call | tf_op jit(solution)/shard_map/write_out/pallas_call | solution.py:417

commit v4 on v3

--- a/solution.py
+++ b/solution.py
@@ -188,14 +188,13 @@
         acc_t[...] = jnp.zeros_like(acc_t)
         wlam = w * lam_col
 
-        @pl.loop(0, gl // gc)
-        def _(c):
-            sl = pl.ds(pl.multiple_of(c * gc, gc), gc)
-            pulled = lax.dot_general(
-                yb[it, 0], fac[0, sl, :], (((1,), (1,)), ((), ())), preferred_element_type=F32
-            ) + lax.dot_general(
-                yb[it, 1], fac[1, sl, :], (((1,), (1,)), ((), ())), preferred_element_type=F32
+        y_t = jnp.concatenate([yb[it, h].astype(F32).T.astype(BF16) for h in range(2)], axis=0)
+        for c in range(gl // gc):
+            sl = pl.ds(c * gc, gc)
+            pulled_t = jnp.dot(fac[0, sl, :], y_t[:half], preferred_element_type=F32) + jnp.dot(
+                fac[1, sl, :], y_t[half:], preferred_element_type=F32
             )
+            pulled = pulled_t.T
             xc = xv[:, sl]
             grad = cost[:, sl] + wlam + pulled + muv[pl.ds(0, rows), sl] - muv[pl.ds(1, rows), sl]
             xn = jnp.clip(xc - TAU * grad, lo[:, sl], hi[:, sl])
@@ -214,6 +213,9 @@
         for cp in rows_out:
             cp.start()
         tot_col = w * jnp.sum(acc_t[...], axis=1, keepdims=True)
+        tot[it, :, pl.ds(0, rows)] = to_row(tot_col)
+        t_copy = send(tot.at[it], tot_x.at[it], t_send.at[it], t_recv.at[it], partner)
+        t_copy.start()
         f_copies = []
         for p in range(2):
             flow[it, p] = jnp.dot(xbb[...], fac[p], preferred_element_type=F32)
@@ -224,10 +226,6 @@
                 )
                 cp.start()
                 f_copies.append(cp)
-        tot[it, :, pl.ds(0, rows)] = to_row(tot_col)
-        t_copy = send(tot.at[it], tot_x.at[it], t_send.at[it], t_recv.at[it], partner)
-        t_copy.start()
-
         for cp in rows_out:
             cp.wait()
         xbv[pl.ds(7, 1), :] = jnp.where(first, pinit[...], xb_prev[it])

time: 57.9 us -> 54.5 us (0.941)
  Pallas kernels: 57.2 us -> 53.8 us
    pallas_call x1, Pallas kernels: 55.4 us -> 52 us  [on_device(): pl.pallas_call(functools.partial(kernel, (ntm, plane, gl_total, hours)),...]
where the time goes in v4:
time: 54.5 us; the launch traced here: 54.4 us
  Pallas kernels  53.8 us (99%)
  between operations  0.65 us (1%)
    pallas_call x1, Pallas kernels, on_device(): pl.pallas_call(functools.partial(kernel, (ntm, plane, gl_total, hours)),...  52 us
    pallas_call x1, Pallas kernels, on_device(): pl.pallas_call(write_out, name='write_out', out_shape=tuple((jax.ShapeDty...  1.76 us

profile of v4, /device:TPU:1, one launch (start us, length us, event | category | flops | bytes accessed | tf_op | source)
XLA Modules:
  0.0 54.4 jit_solution(8338177466461935405)
XLA Ops:
  0.6 52.0 %dispatch_step.1 = (f32[96,4096]{1,0:T(8,128)S(1)}, f32[96,512]{1,0:T(8,128)S(1)}, f32[96,4096]{1,0:T(8,128)S(1)}, f32[1,96]{1,0:T(1,128)S(1)}, f32[2,2]{1,0:T(2,128)S(1)}) custom-call(s32[32,128]{1,0:T(8,128)} %bitcast.10, f32[96,4096]{1,0:T(8,128)} %x_h.1, f32[1,4096]{1,0:T(1,128)} %bitcast.11, f32[1,4096]{1,0:T(1,128)} %bitcast.12, f32[1,4096]{1,0:T(1,128)} %bitcast.13, ...), custom_call_target="tpu_custom_call" | custom-call | tf_op jit(solution)/shard_map/dispatch_step/pallas_call | solution.py:381
  52.6 1.8 %write_out.1 = (f32[96,4096]{1,0:T(8,128)}, f32[96,512]{1,0:T(8,128)}, f32[96,4096]{1,0:T(8,128)}, f32[1,96]{1,0:T(1,128)}, f32[2,2]{1,0:T(2,128)}) custom-call(f32[96,4096]{1,0:T(8,128)S(1)} %get-tuple-element.15.x, f32[96,512]{1,0:T(8,128)S(1)} %get-tuple-element.16.y, f32[96,4096]{1,0:T(8,128)S(1)} %get-tuple-element.17.mu, ...), custom_call_target="tpu_custom_call" | custom-call | tf_op jit(solution)/shard_map/write_out/pallas_call | solution.py:415

commit v5 on v4

--- a/solution.py
+++ b/solution.py
@@ -15,16 +15,17 @@
 MESH = pl.DeviceIdType.MESH
 BF16 = jnp.bfloat16
 F32 = jnp.float32
+STEPS = 32767.0
 
 
 def kernel(
     cfg,
     bus_h, x_h, cost_h, lo_h, hi_h, ramp_h, pinit_h, dem_h, ptdf_h, base_h, lim_h, y_h, mu_h, lam_h,
     xv, yo, muo, lam_o, mov_o,
-    ptdf, table, stage, fac, muv, xbv, xbb, yv, yt, bt, flow, yb, ybs, frecv,
+    ptdf, table, stage, fac, muv, xbv, xbb, yv, yt, bt, flow, yb, ybs, frecv, scale, scale_x,
     bus, cost, lo, hi, ramp, pinit, lim, lim_x, dem, lam, mu_next, xb_prev, xb_next, tot, tot_x,
     acc_p, acc_d, acc_t, msg, ar_a, ar_b,
-    load_sem, ptdf_sem, yb_send, yb_recv, init_send, init_recv, f_send, f_recv, t_send, t_recv,
+    load_sem, ptdf_sem, yb_send, yb_recv, init_send, init_recv, f_send, f_recv, s_send, s_recv, t_send, t_recv,
     ys_send, ys_recv, yr_send, yr_recv, row_send, row_recv, ar_send, ar_recv,
 ):
     ntm, plane, gl_total, hours = cfg
@@ -218,14 +219,25 @@
         t_copy.start()
         f_copies = []
         for p in range(2):
-            flow[it, p] = jnp.dot(xbb[...], fac[p], preferred_element_type=F32)
+            sums_p = jnp.dot(xbb[...], fac[p], preferred_element_type=F32)
             for r, part in enumerate((top, low)):
-                cp = send(
-                    flow.at[it, p, part], frecv.at[it, gen, part], f_send.at[it, p * 2 + r],
-                    f_recv.at[it, gen * 2 + r], (twin, p if r == 0 else 1 - p),
-                )
-                cp.start()
-                f_copies.append(cp)
+                block = sums_p[r * (rows // 2) : (r + 1) * (rows // 2)]
+                largest = jnp.maximum(jnp.max(jnp.abs(block), axis=0, keepdims=True), 1e-30)
+                flow[it, p, part] = jnp.round(block * (STEPS / largest)).astype(jnp.int32).astype(jnp.int16)
+                scale[it, p, r] = largest * (1.0 / STEPS)
+                dev = (twin, p if r == 0 else 1 - p)
+                for cp in (
+                    send(
+                        scale.at[it, p, r], scale_x.at[it, gen, r], s_send.at[it, p * 2 + r],
+                        s_recv.at[it, gen * 2 + r], dev,
+                    ),
+                    send(
+                        flow.at[it, p, part], frecv.at[it, gen, part], f_send.at[it, p * 2 + r],
+                        f_recv.at[it, gen * 2 + r], dev,
+                    ),
+                ):
+                    cp.start()
+                    f_copies.append(cp)
         for cp in rows_out:
             cp.wait()
         xbv[pl.ds(7, 1), :] = jnp.where(first, pinit[...], xb_prev[it])
@@ -261,6 +273,10 @@
         for s in range(2):
             for r, part in enumerate((top, low)):
                 send(
+                    scale.at[it, 0, r], scale_x.at[it, s, r], s_send.at[it, r],
+                    s_recv.at[it, s * 2 + r], (twin, s),
+                ).wait_recv()
+                send(
                     flow.at[it, 0, part], frecv.at[it, s, part], f_send.at[it, r],
                     f_recv.at[it, s * 2 + r], (twin, s),
                 ).wait_recv()
@@ -270,7 +286,9 @@
         half_rows = rows // 2
         for r, part in enumerate((top, low)):
             old = yt[part, :]
-            v = old + SIGMA * (frecv[it, 0, part, :] + frecv[it, 1, part, :])
+            v = old + SIGMA * sum(
+                frecv[it, s, part, :].astype(jnp.int32).astype(F32) * scale_x[it, s, r] for s in range(2)
+            )
             bv = bt[part, :]
             lv = (lim if r == 0 else lim_x)[...]
             yn = v - jnp.clip(v, SIGMA * (bv - lv), SIGMA * (bv + lv))
@@ -395,17 +413,18 @@
             V((rows, half), F32),
             V((rows, half), F32),
             V((rows, half), F32),
-            V((ITERS, 2, rows, half), F32),
+            V((ITERS, 2, rows, half), jnp.int16),
             V((ITERS, 2, rows, half), BF16),
             V((rows, half), BF16),
-            V((ITERS, 2, rows, half), F32),
+            V((ITERS, 2, rows, half), jnp.int16),
+            V((ITERS, 2, 2, 1, half), F32), V((ITERS, 2, 2, 1, half), F32),
             pltpu.SMEM((gl // 128, 128), jnp.int32),
             V((1, gl), F32), V((1, gl), F32), V((1, gl), F32), V((1, gl), F32), V((1, gl), F32),
             V((1, half), F32), V((1, half), F32), V((1, rows), F32), V((1, rows), F32),
             V((1, gl), F32), V((ITERS, 1, gl), F32), V((1, gl), F32), V((ITERS, 1, 128), F32), V((ITERS, 1, 128), F32),
             V((rows, 128), F32), V((rows, 128), F32), V((rows, 128), F32),
             V((2, 1, 128), F32), V((n_a, 1, 128), F32), V((nz, 1, 128), F32),
-            S((12,)), S((2,)), S, S, S((5,)), S((5,)), S((ITERS, 4)), S((ITERS, 4)), S((ITERS,)), S((ITERS,)),
+            S((12,)), S((2,)), S, S, S((5,)), S((5,)), S((ITERS, 4)), S((ITERS, 4)), S((ITERS, 4)), S((ITERS, 4)), S((ITERS,)), S((ITERS,)),
             S((4,)), S((4,)), S((2,)), S((2,)), S((2 * ITERS,)), S((2 * ITERS,)), S((2,)), S((2,)),
         ],
         compiler_params=pltpu.CompilerParams(

time: 54.5 us -> 52.3 us (0.960)
  Pallas kernels: 53.8 us -> 51.6 us
    pallas_call x1, Pallas kernels: 52 us -> 49.8 us  [on_device(): pl.pallas_call(functools.partial(kernel, (ntm, plane, gl_total, hours)),...]
where the time goes in v5:
time: 52.3 us; the launch traced here: 52.2 us
  Pallas kernels  51.6 us (99%)
  between operations  0.65 us (1%)
    pallas_call x1, Pallas kernels, on_device(): pl.pallas_call(functools.partial(kernel, (ntm, plane, gl_total, hours)),...  49.8 us
    pallas_call x1, Pallas kernels, on_device(): pl.pallas_call(write_out, name='write_out', out_shape=tuple((jax.ShapeDty...  1.76 us

profile of v5, /device:TPU:1, one launch (start us, length us, event | category | flops | bytes accessed | tf_op | source)
XLA Modules:
  0.0 52.2 jit_solution(2962832786615287267)
XLA Ops:
  0.6 49.8 %dispatch_step.1 = (f32[96,4096]{1,0:T(8,128)S(1)}, f32[96,512]{1,0:T(8,128)S(1)}, f32[96,4096]{1,0:T(8,128)S(1)}, f32[1,96]{1,0:T(1,128)S(1)}, f32[2,2]{1,0:T(2,128)S(1)}) custom-call(s32[32,128]{1,0:T(8,128)} %bitcast.10, f32[96,4096]{1,0:T(8,128)} %x_h.1, f32[1,4096]{1,0:T(1,128)} %bitcast.11, f32[1,4096]{1,0:T(1,128)} %bitcast.12, f32[1,4096]{1,0:T(1,128)} %bitcast.13, ...), custom_call_target="tpu_custom_call" | custom-call | tf_op jit(solution)/shard_map/dispatch_step/pallas_call | solution.py:399
  50.5 1.8 %write_out.1 = (f32[96,4096]{1,0:T(8,128)}, f32[96,512]{1,0:T(8,128)}, f32[96,4096]{1,0:T(8,128)}, f32[1,96]{1,0:T(1,128)}, f32[2,2]{1,0:T(2,128)}) custom-call(f32[96,4096]{1,0:T(8,128)S(1)} %get-tuple-element.15.x, f32[96,512]{1,0:T(8,128)S(1)} %get-tuple-element.16.y, f32[96,4096]{1,0:T(8,128)S(1)} %get-tuple-element.17.mu, ...), custom_call_target="tpu_custom_call" | custom-call | tf_op jit(solution)/shard_map/write_out/pallas_call | solution.py:434

commit v6 on v5

--- a/solution.py
+++ b/solution.py
@@ -23,7 +23,7 @@
     bus_h, x_h, cost_h, lo_h, hi_h, ramp_h, pinit_h, dem_h, ptdf_h, base_h, lim_h, y_h, mu_h, lam_h,
     xv, yo, muo, lam_o, mov_o,
     ptdf, table, stage, fac, muv, xbv, xbb, yv, yt, bt, flow, yb, ybs, frecv, scale, scale_x,
-    bus, cost, lo, hi, ramp, pinit, lim, lim_x, dem, lam, mu_next, xb_prev, xb_next, tot, tot_x,
+    bus, cost, lo, hi, ramp, pinit, lim, lim_x, dem, lam, mu_next, edge, xb_prev, xb_next, tot, tot_x,
     acc_p, acc_d, acc_t, msg, ar_a, ar_b,
     load_sem, ptdf_sem, yb_send, yb_recv, init_send, init_recv, f_send, f_recv, s_send, s_recv, t_send, t_recv,
     ys_send, ys_recv, yr_send, yr_recv, row_send, row_recv, ar_send, ar_recv,
@@ -57,9 +57,10 @@
         return (lax.rem(zz + d, nz) * plane + in_plane, gen)
 
     nblk = buses // 256
-    per_load = nblk // 2
+    n_load = min(4, nblk)
+    per_load = nblk // n_load
     ptdf_copies = []
-    for c in range(2):
+    for c in range(n_load):
         part = pl.ds(c * per_load * 256, per_load * 256)
         cp = pltpu.make_async_copy(ptdf_h.at[:, part], ptdf.at[:, part], ptdf_sem.at[c])
         cp.start()
@@ -68,13 +69,13 @@
         pltpu.make_async_copy(s, d, load_sem.at[i])
         for i, (s, d) in enumerate(
             [
-                (y_h, yv), (mu_h, muv.at[pl.ds(0, rows)]), (x_h, xv), (cost_h, cost),
+                (mu_h, muv.at[pl.ds(0, rows)]), (x_h, xv), (cost_h, cost), (y_h, yv),
                 (lo_h, lo), (hi_h, hi), (ramp_h, ramp), (pinit_h, pinit), (lim_h, lim), (dem_h, dem),
                 (lam_h, lam), (bus_h, bus),
             ]
         )
     ]
-    for cp in loads:
+    for cp in loads[3:]:
         cp.start()
 
     barrier = pltpu.get_barrier_semaphore()
@@ -97,24 +98,15 @@
 
     nlb = lines // 128
     flat = table.reshape(buses * nlb, 128)
-    eye = (
-        lax.broadcasted_iota(jnp.int32, (256, 256), 0)
-        == lax.broadcasted_iota(jnp.int32, (256, 256), 1)
-    ).astype(BF16)
     for c in range(nblk):
         if c % per_load == 0:
             ptdf_copies[c // per_load].wait()
-        turned = lax.dot_general(
-            eye, ptdf[:, c * 256 : (c + 1) * 256], (((1,), (1,)), ((), ())),
-            preferred_element_type=F32,
-        )
+            if c // per_load == n_load - 1:
+                for cp in loads[:3]:
+                    cp.start()
+        turned = ptdf[:, c * 256 : (c + 1) * 256].T.astype(F32)
         for j in range(nlb):
             flat[pl.ds(c * 256 * nlb + j, 256, stride=nlb), :] = turned[:, j * 128 : (j + 1) * 128]
-
-    for cp in loads:
-        cp.wait()
-    yb[0, gen] = yv[...].astype(BF16)
-    pl.semaphore_wait(barrier, n_a - 1 + nz - 1 + 4)
 
     def send(src, dst, ssem, rsem, dev):
         return pltpu.make_async_remote_copy(
@@ -126,10 +118,44 @@
             src, dst, row_send.at[k], row_recv.at[k], device_id=dev, device_id_type=MESH
         )
 
+    group = 16
+    n_group = 128 // group
+
+    def gather(i):
+        def fetch(s, k):
+            stage[pl.ds((s * group + k) * nlb, nlb), :] = table[bus[i, s * group + k]]
+
+        def pack(s, j):
+            g0 = pl.multiple_of(i * 128 + s * group, group)
+            got = stage[pl.ds(s * group * nlb + j, group, stride=nlb), :]
+            fac[j // (nlb // 2), pl.ds(g0, group), pl.ds((j % (nlb // 2)) * 128, 128)] = got.astype(BF16)
+
+        for k in range(group):
+            fetch(0, k)
+        for s in range(n_group):
+            per = group // nlb
+            for j in range(nlb):
+                if s + 1 < n_group:
+                    for k in range(per):
+                        fetch(s + 1, j * per + k)
+                pack(s, j)
+
+    steps = gl // 128
+    for cp in loads[3:]:
+        cp.wait()
+    pl.loop(0, steps // 8)(gather)
+    yb[0, gen] = yv[...].astype(BF16)
+    pl.semaphore_wait(barrier, n_a - 1 + nz - 1 + 4)
+
     yb_copy = send(yb.at[0, gen], yb.at[0, gen], yb_send, yb_recv, partner)
     yb_copy.start()
-    mu_copy = send_row(0, muv.at[pl.ds(0, 1)], mu_next, prv)
-    mu_copy.start()
+    mu_copy = send_row(0, mu_h.at[pl.ds(0, 1)], mu_next, prv)
+
+    @pl.when(tm > 0)
+    def _():
+        mu_copy.start()
+
+    pl.loop(steps // 8, steps // 2)(gather)
     moves = [
         send(src.at[part], dst.at[part], init_send.at[i], init_recv.at[i], (twin, dev))
         for i, (src, dst, part, dev) in enumerate(
@@ -140,28 +166,9 @@
     for cp in moves:
         cp.start()
 
-    group = 16
-    n_group = 128 // group
-
-    @pl.loop(0, gl // 128)
-    def _(i):
-        def fetch(s, k):
-            stage[pl.ds((s * group + k) * nlb, nlb), :] = table[bus[i, s * group + k]]
-
-        def pack(s, j):
-            g0 = pl.multiple_of(i * 128 + s * group, group)
-            got = stage[pl.ds(s * group * nlb + j, group, stride=nlb), :]
-            fac[j // (nlb // 2), pl.ds(g0, group), pl.ds((j % (nlb // 2)) * 128, 128)] = got.astype(BF16)
-
-        for k in range(group):
-            fetch(0, k)
-        for s in range(n_group):
-            per = group // nlb
-            for j in range(nlb):
-                if s + 1 < n_group:
-                    for k in range(per):
-                        fetch(s + 1, j * per + k)
-                pack(s, j)
+    pl.loop(steps // 2, steps)(gather)
+    for cp in loads[:3]:
+        cp.wait()
 
     eye_r = lax.broadcasted_iota(jnp.int32, (rows, rows), 0) == lax.broadcasted_iota(
         jnp.int32, (rows, rows), 1
@@ -178,7 +185,15 @@
     lam_col = to_column(lam[...])
     dem_col = to_column(dem[...])
     yb_copy.wait()
-    mu_copy.wait()
+
+    @pl.when(tm > 0)
+    def _():
+        mu_copy.wait_send()
+
+    @pl.when(tm < ntm - 1)
+    def _():
+        mu_copy.wait_recv()
+
     muv[pl.ds(rows, 1), :] = jnp.where(last, 0.0, mu_next[...])
 
     gc = 512
@@ -204,15 +219,28 @@
             d2 = d * d
             xv[:, sl] = xn
             xbv[pl.ds(8, rows), sl] = xb
+            edge[it, 0, :, sl] = xb[rows - 1 :]
+            if it < ITERS - 1:
+                edge[it, 1, :, sl] = xb[:1]
             xbb[:, sl] = xb.astype(BF16)
             acc_p[...] += sum(d2[:, k * 128 : (k + 1) * 128] for k in range(gc // 128))
             acc_t[...] += sum(xb[:, k * 128 : (k + 1) * 128] for k in range(gc // 128))
 
-        rows_out = [send_row(1 + 2 * it, xbv.at[pl.ds(8 + rows - 1, 1)], xb_prev.at[it], nxt)]
+        rows_out = [send_row(1 + 2 * it, edge.at[it, 0], xb_prev.at[it], nxt)]
         if it < ITERS - 1:
-            rows_out.append(send_row(2 + 2 * it, xbv.at[pl.ds(8, 1)], xb_next, prv))
-        for cp in rows_out:
-            cp.start()
+            rows_out.append(send_row(2 + 2 * it, edge.at[it, 1], xb_next, prv))
+        has = [tm < ntm - 1, tm > 0]
+
+        @pl.when(has[0])
+        def _():
+            rows_out[0].start()
+
+        if it < ITERS - 1:
+
+            @pl.when(has[1])
+            def _():
+                rows_out[1].start()
+
         tot_col = w * jnp.sum(acc_t[...], axis=1, keepdims=True)
         tot[it, :, pl.ds(0, rows)] = to_row(tot_col)
         t_copy = send(tot.at[it], tot_x.at[it], t_send.at[it], t_recv.at[it], partner)
@@ -238,30 +266,43 @@
                 ):
                     cp.start()
                     f_copies.append(cp)
-        for cp in rows_out:
-            cp.wait()
-        xbv[pl.ds(7, 1), :] = jnp.where(first, pinit[...], xb_prev[it])
-        if it < ITERS - 1:
-            m_n = muv[pl.ds(rows, 1), :]
-            u_n = m_n + SIGMA * (xb_next[...] - xbv[pl.ds(8 + rows - 1, 1), :])
-            mn_n = u_n - jnp.clip(u_n, -SIGMA * ramp[...], SIGMA * ramp[...])
-            muv[pl.ds(rows, 1), :] = jnp.where(last, 0.0, mn_n)
-
-        @pl.loop(0, gl // gc)
-        def _(c):
-            sl = pl.ds(pl.multiple_of(c * gc, gc), gc)
-            m = muv[pl.ds(0, rows), sl]
-            u = m + SIGMA * (xbv[pl.ds(8, rows), sl] - xbv[pl.ds(7, rows), sl])
-            r = SIGMA * ramp[:, sl]
-            mn = u - jnp.clip(u, -r, r)
+        def ramp_pass():
+            @pl.when(has[0])
+            def _():
+                rows_out[0].wait_send()
+                if it < ITERS - 1:
+                    rows_out[1].wait_recv()
+
+            @pl.when(has[1])
+            def _():
+                rows_out[0].wait_recv()
+                if it < ITERS - 1:
+                    rows_out[1].wait_send()
+
+            xbv[pl.ds(7, 1), :] = jnp.where(first, pinit[...], xb_prev[it])
             if it < ITERS - 1:
-                muv[pl.ds(0, rows), sl] = mn
-            else:
-                muo[:, sl] = mn
-            d = mn - m
-            d2 = d * d
-            acc_d[...] += sum(d2[:, k * 128 : (k + 1) * 128] for k in range(gc // 128))
-
+                m_n = muv[pl.ds(rows, 1), :]
+                u_n = m_n + SIGMA * (xb_next[...] - xbv[pl.ds(8 + rows - 1, 1), :])
+                mn_n = u_n - jnp.clip(u_n, -SIGMA * ramp[...], SIGMA * ramp[...])
+                muv[pl.ds(rows, 1), :] = jnp.where(last, 0.0, mn_n)
+
+            @pl.loop(0, gl // gc)
+            def _(c):
+                sl = pl.ds(pl.multiple_of(c * gc, gc), gc)
+                m = muv[pl.ds(0, rows), sl]
+                u = m + SIGMA * (xbv[pl.ds(8, rows), sl] - xbv[pl.ds(7, rows), sl])
+                r = SIGMA * ramp[:, sl]
+                mn = u - jnp.clip(u, -r, r)
+                if it < ITERS - 1:
+                    muv[pl.ds(0, rows), sl] = mn
+                else:
+                    muo[:, sl] = mn
+                d = mn - m
+                d2 = d * d
+                acc_d[...] += sum(d2[:, k * 128 : (k + 1) * 128] for k in range(gc // 128))
+
+        if it == ITERS - 1:
+            ramp_pass()
         t_copy.wait()
         totals = tot_col + to_column(tot_x[it, :, pl.ds(0, rows)])
         lam_new = lam_col + SIGMA * (totals - dem_col)
@@ -305,6 +346,8 @@
             acc_d[pl.ds(r * half_rows, half_rows), :] += sum(
                 dy2[:, k * 128 : (k + 1) * 128] for k in range(half // 128)
             )
+        if it < ITERS - 1:
+            ramp_pass()
         primal = jnp.sum(acc_p[...], keepdims=True) / (TAU * cells)
         dual = (
             jnp.sum(acc_d[...], keepdims=True)
@@ -421,10 +464,10 @@
             pltpu.SMEM((gl // 128, 128), jnp.int32),
             V((1, gl), F32), V((1, gl), F32), V((1, gl), F32), V((1, gl), F32), V((1, gl), F32),
             V((1, half), F32), V((1, half), F32), V((1, rows), F32), V((1, rows), F32),
-            V((1, gl), F32), V((ITERS, 1, gl), F32), V((1, gl), F32), V((ITERS, 1, 128), F32), V((ITERS, 1, 128), F32),
+            V((1, gl), F32), V((ITERS, 2, 1, gl), F32), V((ITERS, 1, gl), F32), V((1, gl), F32), V((ITERS, 1, 128), F32), V((ITERS, 1, 128), F32),
             V((rows, 128), F32), V((rows, 128), F32), V((rows, 128), F32),
             V((2, 1, 128), F32), V((n_a, 1, 128), F32), V((nz, 1, 128), F32),
-            S((12,)), S((2,)), S, S, S((5,)), S((5,)), S((ITERS, 4)), S((ITERS, 4)), S((ITERS, 4)), S((ITERS, 4)), S((ITERS,)), S((ITERS,)),
+            S((12,)), S((4,)), S, S, S((5,)), S((5,)), S((ITERS, 4)), S((ITERS, 4)), S((ITERS, 4)), S((ITERS, 4)), S((ITERS,)), S((ITERS,)),
             S((4,)), S((4,)), S((2,)), S((2,)), S((2 * ITERS,)), S((2 * ITERS,)), S((2,)), S((2,)),
         ],
         compiler_params=pltpu.CompilerParams(

time: 52.3 us -> 51 us (0.975)
  Pallas kernels: 51.6 us -> 50.3 us
    pallas_call x1, Pallas kernels: 49.8 us -> 48.5 us  [on_device(): pl.pallas_call(functools.partial(kernel, (ntm, plane, gl_total, hours)),...]
where the time goes in v6:
time: 51 us; the launch traced here: 50.9 us
  Pallas kernels  50.3 us (99%)
  between operations  0.65 us (1%)
    pallas_call x1, Pallas kernels, on_device(): pl.pallas_call(functools.partial(kernel, (ntm, plane, gl_total, hours)),...  48.5 us
    pallas_call x1, Pallas kernels, on_device(): pl.pallas_call(write_out, name='write_out', out_shape=tuple((jax.ShapeDty...  1.76 us

profile of v6, /device:TPU:1, one launch (start us, length us, event | category | flops | bytes accessed | tf_op | source)
XLA Modules:
  0.0 50.9 jit_solution(3076058989069974846)
XLA Ops:
  0.6 48.5 %dispatch_step.1 = (f32[96,4096]{1,0:T(8,128)S(1)}, f32[96,512]{1,0:T(8,128)S(1)}, f32[96,4096]{1,0:T(8,128)S(1)}, f32[1,96]{1,0:T(1,128)S(1)}, f32[2,2]{1,0:T(2,128)S(1)}) custom-call(s32[32,128]{1,0:T(8,128)} %bitcast.10, f32[96,4096]{1,0:T(8,128)} %x_h.1, f32[1,4096]{1,0:T(1,128)} %bitcast.11, f32[1,4096]{1,0:T(1,128)} %bitcast.12, f32[1,4096]{1,0:T(1,128)} %bitcast.13, ...), custom_call_target="tpu_custom_call" | custom-call | tf_op jit(solution)/shard_map/dispatch_step/pallas_call | solution.py:442
  49.2 1.8 %write_out.1 = (f32[96,4096]{1,0:T(8,128)}, f32[96,512]{1,0:T(8,128)}, f32[96,4096]{1,0:T(8,128)}, f32[1,96]{1,0:T(1,128)}, f32[2,2]{1,0:T(2,128)}) custom-call(f32[96,4096]{1,0:T(8,128)S(1)} %get-tuple-element.15.x, f32[96,512]{1,0:T(8,128)S(1)} %get-tuple-element.16.y, f32[96,4096]{1,0:T(8,128)S(1)} %get-tuple-element.17.mu, ...), custom_call_target="tpu_custom_call" | custom-call | tf_op jit(solution)/shard_map/write_out/pallas_call | solution.py:477

commit v7 on v6

--- a/solution.py
+++ b/solution.py
@@ -23,7 +23,7 @@
     bus_h, x_h, cost_h, lo_h, hi_h, ramp_h, pinit_h, dem_h, ptdf_h, base_h, lim_h, y_h, mu_h, lam_h,
     xv, yo, muo, lam_o, mov_o,
     ptdf, table, stage, fac, muv, xbv, xbb, yv, yt, bt, flow, yb, ybs, frecv, scale, scale_x,
-    bus, cost, lo, hi, ramp, pinit, lim, lim_x, dem, lam, mu_next, edge, xb_prev, xb_next, tot, tot_x,
+    bus, cost, lo, hi, ramp, pinit, lim, lim_x, lims, dem, lam, mu_next, edge, xb_prev, xb_next, tot, tot_x,
     acc_p, acc_d, acc_t, msg, ar_a, ar_b,
     load_sem, ptdf_sem, yb_send, yb_recv, init_send, init_recv, f_send, f_recv, s_send, s_recv, t_send, t_recv,
     ys_send, ys_recv, yr_send, yr_recv, row_send, row_recv, ar_send, ar_recv,
@@ -257,11 +257,11 @@
                 for cp in (
                     send(
                         scale.at[it, p, r], scale_x.at[it, gen, r], s_send.at[it, p * 2 + r],
-                        s_recv.at[it, gen * 2 + r], dev,
+                        s_recv.at[it, gen * 2 + p], dev,
                     ),
                     send(
                         flow.at[it, p, part], frecv.at[it, gen, part], f_send.at[it, p * 2 + r],
-                        f_recv.at[it, gen * 2 + r], dev,
+                        f_recv.at[it, gen * 2 + p], dev,
                     ),
                 ):
                     cp.start()
@@ -311,39 +311,42 @@
 
         for cp in f_copies:
             cp.wait_send()
-        for s in range(2):
-            for r, part in enumerate((top, low)):
-                send(
-                    scale.at[it, 0, r], scale_x.at[it, s, r], s_send.at[it, r],
-                    s_recv.at[it, s * 2 + r], (twin, s),
-                ).wait_recv()
-                send(
-                    flow.at[it, 0, part], frecv.at[it, s, part], f_send.at[it, r],
-                    f_recv.at[it, s * 2 + r], (twin, s),
-                ).wait_recv()
         if it == 0:
             for cp in moves:
                 cp.wait()
+            lims[other] = lim_x[...]
+            lims[gen] = lim[...]
         half_rows = rows // 2
-        for r, part in enumerate((top, low)):
+        for p in range(2):
+            r = gen if p == 0 else other
+            part = pl.ds(pl.multiple_of(r * half_rows, half_rows), half_rows)
+            for s in range(2):
+                send(
+                    scale.at[it, 0, 0], scale_x.at[it, s, r], s_send.at[it, 0], s_recv.at[it, s * 2 + p],
+                    (twin, s),
+                ).wait_recv()
+                send(
+                    flow.at[it, 0, top], frecv.at[it, s, part], f_send.at[it, 0], f_recv.at[it, s * 2 + p],
+                    (twin, s),
+                ).wait_recv()
             old = yt[part, :]
             v = old + SIGMA * sum(
                 frecv[it, s, part, :].astype(jnp.int32).astype(F32) * scale_x[it, s, r] for s in range(2)
             )
             bv = bt[part, :]
-            lv = (lim if r == 0 else lim_x)[...]
+            lv = lims[p]
             yn = v - jnp.clip(v, SIGMA * (bv - lv), SIGMA * (bv + lv))
             yt[part, :] = yn
             if it < ITERS - 1:
                 ybs[part, :] = yn.astype(BF16)
                 for dev in range(2):
                     send(
-                        ybs.at[part], yb.at[it + 1, gen if r == 0 else other, part],
-                        ys_send.at[dev * 2 + r], ys_recv.at[gen * 2 + r], (twin, dev),
+                        ybs.at[part], yb.at[it + 1, p, part], ys_send.at[dev * 2 + p],
+                        ys_recv.at[gen * 2 + p], (twin, dev),
                     ).start()
             dy = yn - old
             dy2 = dy * dy
-            acc_d[pl.ds(r * half_rows, half_rows), :] += sum(
+            acc_d[pl.ds(0, half_rows), :] += sum(
                 dy2[:, k * 128 : (k + 1) * 128] for k in range(half // 128)
             )
         if it < ITERS - 1:
@@ -356,11 +359,11 @@
         sums += [primal, dual]
         if it < ITERS - 1:
             for s in range(2):
-                for r, part in enumerate((top, low)):
-                    piece = s if r == 0 else 1 - s
+                for p in range(2):
+                    part = top if s == p else low
                     send(
-                        ybs.at[part], yb.at[it + 1, piece, part], ys_send.at[s * 2 + r],
-                        ys_recv.at[s * 2 + r], (twin, s),
+                        ybs.at[part], yb.at[it + 1, p, part], ys_send.at[s * 2 + p],
+                        ys_recv.at[s * 2 + p], (twin, s),
                     ).wait()
 
     lane = lax.broadcasted_iota(jnp.int32, (1, 128), 1)
@@ -463,7 +466,7 @@
             V((ITERS, 2, 2, 1, half), F32), V((ITERS, 2, 2, 1, half), F32),
             pltpu.SMEM((gl // 128, 128), jnp.int32),
             V((1, gl), F32), V((1, gl), F32), V((1, gl), F32), V((1, gl), F32), V((1, gl), F32),
-            V((1, half), F32), V((1, half), F32), V((1, rows), F32), V((1, rows), F32),
+            V((1, half), F32), V((1, half), F32), V((2, 1, half), F32), V((1, rows), F32), V((1, rows), F32),
             V((1, gl), F32), V((ITERS, 2, 1, gl), F32), V((ITERS, 1, gl), F32), V((1, gl), F32), V((ITERS, 1, 128), F32), V((ITERS, 1, 128), F32),
             V((rows, 128), F32), V((rows, 128), F32), V((rows, 128), F32),
             V((2, 1, 128), F32), V((n_a, 1, 128), F32), V((nz, 1, 128), F32),

time: 51 us -> 50.4 us (0.988)
  Pallas kernels: 50.3 us -> 49.7 us
    pallas_call x1, Pallas kernels: 48.5 us -> 47.9 us  [on_device(): pl.pallas_call(functools.partial(kernel, (ntm, plane, gl_total, hours)),...]
where the time goes in v7:
time: 50.4 us; the launch traced here: 50.3 us
  Pallas kernels  49.7 us (99%)
  between operations  0.65 us (1%)
    pallas_call x1, Pallas kernels, on_device(): pl.pallas_call(functools.partial(kernel, (ntm, plane, gl_total, hours)),...  47.9 us
    pallas_call x1, Pallas kernels, on_device(): pl.pallas_call(write_out, name='write_out', out_shape=tuple((jax.ShapeDty...  1.76 us

profile of v7, /device:TPU:1, one launch (start us, length us, event | category | flops | bytes accessed | tf_op | source)
XLA Modules:
  0.0 50.3 jit_solution(12947964745065279453)
XLA Ops:
  0.6 47.9 %dispatch_step.1 = (f32[96,4096]{1,0:T(8,128)S(1)}, f32[96,512]{1,0:T(8,128)S(1)}, f32[96,4096]{1,0:T(8,128)S(1)}, f32[1,96]{1,0:T(1,128)S(1)}, f32[2,2]{1,0:T(2,128)S(1)}) custom-call(s32[32,128]{1,0:T(8,128)} %bitcast.10, f32[96,4096]{1,0:T(8,128)} %x_h.1, f32[1,4096]{1,0:T(1,128)} %bitcast.11, f32[1,4096]{1,0:T(1,128)} %bitcast.12, f32[1,4096]{1,0:T(1,128)} %bitcast.13, ...), custom_call_target="tpu_custom_call" | custom-call | tf_op jit(solution)/shard_map/dispatch_step/pallas_call | solution.py:445
  48.6 1.8 %write_out.1 = (f32[96,4096]{1,0:T(8,128)}, f32[96,512]{1,0:T(8,128)}, f32[96,4096]{1,0:T(8,128)}, f32[1,96]{1,0:T(1,128)}, f32[2,2]{1,0:T(2,128)}) custom-call(f32[96,4096]{1,0:T(8,128)S(1)} %get-tuple-element.15.x, f32[96,512]{1,0:T(8,128)S(1)} %get-tuple-element.16.y, f32[96,4096]{1,0:T(8,128)S(1)} %get-tuple-element.17.mu, ...), custom_call_target="tpu_custom_call" | custom-call | tf_op jit(solution)/shard_map/write_out/pallas_call | solution.py:480

commit v8 on v7

--- a/solution.py
+++ b/solution.py
@@ -198,6 +198,7 @@
 
     gc = 512
     sums = []
+    late = []
     for it in range(ITERS):
         acc_p[...] = jnp.zeros_like(acc_p)
         acc_d[...] = jnp.zeros_like(acc_d)
@@ -303,14 +304,6 @@
 
         if it == ITERS - 1:
             ramp_pass()
-        t_copy.wait()
-        totals = tot_col + to_column(tot_x[it, :, pl.ds(0, rows)])
-        lam_new = lam_col + SIGMA * (totals - dem_col)
-        dl = lam_new - lam_col
-        lam_col = lam_new
-
-        for cp in f_copies:
-            cp.wait_send()
         if it == 0:
             for cp in moves:
                 cp.wait()
@@ -349,6 +342,12 @@
             acc_d[pl.ds(0, half_rows), :] += sum(
                 dy2[:, k * 128 : (k + 1) * 128] for k in range(half // 128)
             )
+        t_copy.wait()
+        totals = tot_col + to_column(tot_x[it, :, pl.ds(0, rows)])
+        lam_new = lam_col + SIGMA * (totals - dem_col)
+        dl = lam_new - lam_col
+        lam_col = lam_new
+        late += f_copies
         if it < ITERS - 1:
             ramp_pass()
         primal = jnp.sum(acc_p[...], keepdims=True) / (TAU * cells)
@@ -361,10 +360,12 @@
             for s in range(2):
                 for p in range(2):
                     part = top if s == p else low
-                    send(
+                    cp = send(
                         ybs.at[part], yb.at[it + 1, p, part], ys_send.at[s * 2 + p],
                         ys_recv.at[s * 2 + p], (twin, s),
-                    ).wait()
+                    )
+                    cp.wait_recv()
+                    late.append(cp)
 
     lane = lax.broadcasted_iota(jnp.int32, (1, 128), 1)
     packed = jnp.zeros((1, 128), F32)
@@ -385,7 +386,6 @@
         if between is not None:
             between()
         several = buf.at[pl.ds(0, n - 1)]
-        pltpu.make_async_copy(several, several, ar_send.at[k]).wait()
         pltpu.make_async_copy(several, several, ar_recv.at[k]).wait()
         return jnp.sum(buf[...], axis=0)
 
@@ -411,6 +411,11 @@
     lam_o[...] = to_row(lam_col)
     for cp in y_back:
         cp.wait()
+    for cp in late:
+        cp.wait_send()
+    for k, (buf, n) in enumerate(((ar_a, n_a), (ar_b, nz))):
+        several = buf.at[pl.ds(0, n - 1)]
+        pltpu.make_async_copy(several, several, ar_send.at[k]).wait()
 
 
 def write_out(x, y, mu, lam, mov, x_h, y_h, mu_h, lam_h, mov_h, sem):

time: 50.4 us -> 50.5 us (level)
  no operation moved by 1% of the time
where the time goes in v8:
time: 50.5 us; the launch traced here: 50.4 us
  Pallas kernels  49.8 us (99%)
  between operations  0.65 us (1%)
    pallas_call x1, Pallas kernels, on_device(): pl.pallas_call(functools.partial(kernel, (ntm, plane, gl_total, hours)),...  48 us
    pallas_call x1, Pallas kernels, on_device(): pl.pallas_call(write_out, name='write_out', out_shape=tuple((jax.ShapeDty...  1.76 us

profile of v8, /device:TPU:1, one launch (start us, length us, event | category | flops | bytes accessed | tf_op | source)
XLA Modules:
  0.0 50.4 jit_solution(5269201270249455716)
XLA Ops:
  0.6 48.0 %dispatch_step.1 = (f32[96,4096]{1,0:T(8,128)S(1)}, f32[96,512]{1,0:T(8,128)S(1)}, f32[96,4096]{1,0:T(8,128)S(1)}, f32[1,96]{1,0:T(1,128)S(1)}, f32[2,2]{1,0:T(2,128)S(1)}) custom-call(s32[32,128]{1,0:T(8,128)} %bitcast.10, f32[96,4096]{1,0:T(8,128)} %x_h.1, f32[1,4096]{1,0:T(1,128)} %bitcast.11, f32[1,4096]{1,0:T(1,128)} %bitcast.12, f32[1,4096]{1,0:T(1,128)} %bitcast.13, ...), custom_call_target="tpu_custom_call" | custom-call | tf_op jit(solution)/shard_map/dispatch_step/pallas_call | solution.py:450
  48.7 1.8 %write_out.1 = (f32[96,4096]{1,0:T(8,128)}, f32[96,512]{1,0:T(8,128)}, f32[96,4096]{1,0:T(8,128)}, f32[1,96]{1,0:T(1,128)}, f32[2,2]{1,0:T(2,128)}) custom-call(f32[96,4096]{1,0:T(8,128)S(1)} %get-tuple-element.15.x, f32[96,512]{1,0:T(8,128)S(1)} %get-tuple-element.16.y, f32[96,4096]{1,0:T(8,128)S(1)} %get-tuple-element.17.mu, ...), custom_call_target="tpu_custom_call" | custom-call | tf_op jit(solution)/shard_map/write_out/pallas_call | solution.py:485

commit v9 on v8

--- a/solution.py
+++ b/solution.py
@@ -196,7 +196,7 @@
 
     muv[pl.ds(rows, 1), :] = jnp.where(last, 0.0, mu_next[...])
 
-    gc = 512
+    gc = 1024
     sums = []
     late = []
     for it in range(ITERS):

time: 50.5 us -> 50.7 us (level)
  no operation moved by 1% of the time
where the time goes in v9:
time: 50.7 us; the launch traced here: 50.6 us
  Pallas kernels  49.9 us (98%)
  between operations  0.65 us (1%)
    pallas_call x1, Pallas kernels, on_device(): pl.pallas_call(functools.partial(kernel, (ntm, plane, gl_total, hours)),...  48.2 us
    pallas_call x1, Pallas kernels, on_device(): pl.pallas_call(write_out, name='write_out', out_shape=tuple((jax.ShapeDty...  1.76 us

profile of v9, /device:TPU:1, one launch (start us, length us, event | category | flops | bytes accessed | tf_op | source)
XLA Modules:
  0.0 50.6 jit_solution(15933307899494618542)
XLA Ops:
  0.6 48.2 %dispatch_step.1 = (f32[96,4096]{1,0:T(8,128)S(1)}, f32[96,512]{1,0:T(8,128)S(1)}, f32[96,4096]{1,0:T(8,128)S(1)}, f32[1,96]{1,0:T(1,128)S(1)}, f32[2,2]{1,0:T(2,128)S(1)}) custom-call(s32[32,128]{1,0:T(8,128)} %bitcast.10, f32[96,4096]{1,0:T(8,128)} %x_h.1, f32[1,4096]{1,0:T(1,128)} %bitcast.11, f32[1,4096]{1,0:T(1,128)} %bitcast.12, f32[1,4096]{1,0:T(1,128)} %bitcast.13, ...), custom_call_target="tpu_custom_call" | custom-call | tf_op jit(solution)/shard_map/dispatch_step/pallas_call | solution.py:450
  48.8 1.8 %write_out.1 = (f32[96,4096]{1,0:T(8,128)}, f32[96,512]{1,0:T(8,128)}, f32[96,4096]{1,0:T(8,128)}, f32[1,96]{1,0:T(1,128)}, f32[2,2]{1,0:T(2,128)}) custom-call(f32[96,4096]{1,0:T(8,128)S(1)} %get-tuple-element.15.x, f32[96,512]{1,0:T(8,128)S(1)} %get-tuple-element.16.y, f32[96,4096]{1,0:T(8,128)S(1)} %get-tuple-element.17.mu, ...), custom_call_target="tpu_custom_call" | custom-call | tf_op jit(solution)/shard_map/write_out/pallas_call | solution.py:485
